TPU v7x, 32 devices: a whole 2x2x4 slice. The times are simulated.
32 devices in a mesh: dp: 16 (over z, x, core), tensor: 2 (over y).
Axes of the slice: x: 2, y: 2, z: 4, core: 2. Of those that a mesh axis runs over, the one named last changes fastest.
Arguments:
- hidden: bfloat16 [5120, 18432], P('dp', 'tensor'), may hold values from -6 to 6
- fixed_down_weight: bfloat16 [18432, 4608], P('tensor', 'dp'), may hold values from -4 to 4
- lowrank_factor_b: bfloat16 [18432, 16], P('tensor'), may hold values from -0.046875 to 0.046875
- lowrank_factor_a: bfloat16 [16, 4608], P(None, 'dp'), may hold values from -1.5 to 1.5
- magnitude: float32 [4608], P('tensor'), may hold values from 0.5 to 2
- cotangent: bfloat16 [5120, 4608], P('dp', 'tensor'), may hold values from -0.083496094 to 0.083496094
Outputs:
- mixed: bfloat16 [5120, 4608], P('dp', 'tensor')
- gradient_column_scale: float32 [4608], P(('tensor', 'dp'))
- gradient_factor_a: float32 [16, 4608], P(None, ('tensor', 'dp'))
- gradient_factor_b: float32 [18432, 16], P(('tensor', 'dp'))
All inputs are finite; a program needn't handle non-finite values.
Results may differ from a plain program's by a relative error of at most 0.0054.
Values may be sent and summed in bfloat16 or wider, within the bound.
A program may use at most 192 MiB of HBM per device.

v0:
```python
import jax
import jax.numpy as jnp
from jax import lax
from jax.sharding import Mesh, PartitionSpec as P

F32, BF16 = jnp.float32, jnp.bfloat16


def body(hidden, weight, factor_b, factor_a, magnitude, cotangent, *, n_out, n_in, n_t):
    rows, depth = hidden.shape
    cols = weight.shape[1]
    rank = factor_b.shape[1]
    out_cols = magnitude.shape[0]
    group = 2 * n_in
    dp = ("outer", "mid", "core")
    outer = lax.axis_index("outer")
    place = lax.axis_index("mid") * 2 + lax.axis_index("core")
    own = lax.axis_index("tensor")

    swap_mid = [(i, (i + 1) % n_in) for i in range(n_in)]
    swap_core = [(0, 1), (1, 0)]
    h_mid = lax.ppermute(hidden, "mid", swap_mid)
    w_all = lax.all_gather(weight, "outer", axis=1, tiled=True)
    h_core = lax.ppermute(hidden, "core", swap_core)
    h_both = lax.ppermute(h_mid, "core", swap_core)

    low_part = jnp.dot(hidden, factor_b, preferred_element_type=F32)
    merged = weight.astype(F32) + jnp.dot(factor_b, factor_a, preferred_element_type=F32)
    local_sq = jnp.sum(merged * merged, axis=0)
    low, block_sq = lax.psum((low_part, local_sq), "tensor")
    col_sq = lax.all_gather(block_sq, dp, axis=0, tiled=True)
    full_a = lax.all_gather(factor_a, dp, axis=1, tiled=True)
    norms = jnp.sqrt(lax.dynamic_slice_in_dim(col_sq, own * out_cols, out_cols, 0) + 1e-06)
    scale = magnitude / norms
    low_b = low.astype(BF16)
    own_a = lax.dynamic_slice_in_dim(full_a, own * out_cols, out_cols, 1)
    adapter = jnp.dot(low_b, own_a, preferred_element_type=F32)

    h_all = jnp.zeros((group, rows, depth), BF16)
    for block, flip in ((hidden, 0), (h_core, 1), (h_mid, 2), (h_both, 3)):
        h_all = lax.dynamic_update_slice_in_dim(h_all, block[None], place ^ flip, 0)
    h_rows = h_all.reshape(group * rows, depth)

    cot = cotangent.astype(F32)
    dpre_b = (cot * scale).astype(BF16)
    back_b = lax.psum(jnp.dot(dpre_b, own_a.T, preferred_element_type=F32), "tensor").astype(BF16)
    b_part = jnp.dot(back_b.T, hidden, preferred_element_type=F32)
    a_part = jnp.dot(low_b.T, dpre_b, preferred_element_type=F32)
    n_dp = n_out * group
    parts = jnp.concatenate([x.reshape(rank, n_dp, -1) for x in (a_part, b_part)], axis=2)
    parts = lax.all_to_all(parts.transpose(1, 0, 2), dp, 0, 0, tiled=True)
    sums = jnp.sum(parts, axis=0)
    grad_a = sums[:, : out_cols // n_dp]
    grad_b = sums[:, out_cols // n_dp :].T
    w_all, grad_a, grad_b = lax.optimization_barrier((w_all, grad_a, grad_b))

    per_t = n_out // n_t
    sends = jnp.dot(h_rows, w_all, preferred_element_type=F32).astype(BF16)
    sends = sends.reshape(group, rows, n_t, per_t, cols).transpose(2, 0, 3, 1, 4)
    sends = sends.reshape(n_t * group, per_t, rows, cols)
    got = lax.all_to_all(sends, ("tensor", "mid", "core"), 0, 0, tiled=True)
    got = got.reshape(n_t, group, per_t, rows, cols)
    summed = jnp.sum(got.astype(F32), axis=0).transpose(2, 1, 0, 3).reshape(rows, out_cols)

    pre = summed + adapter
    mixed = (pre * scale).astype(BF16)
    mag_part = jnp.sum(cot * pre, axis=0) / norms
    for axis in ("core", "mid", "outer"):
        mag_part = lax.psum(mag_part, axis)
    at = (outer * group + place) * (out_cols // n_dp)
    grad_scale = lax.dynamic_slice_in_dim(mag_part, at, out_cols // n_dp, 0)
    return mixed, grad_scale, grad_a, grad_b


def solution(mesh):
    n_dp, n_t = mesh.shape["dp"], mesh.shape["tensor"]
    n_in = 2
    n_out = n_dp // (2 * n_in)
    fine = Mesh(mesh.devices.reshape(n_out, n_in, 2, n_t), ("outer", "mid", "core", "tensor"))
    dp = ("outer", "mid", "core")

    def step(*args):
        return body(*args, n_out=n_out, n_in=n_in, n_t=n_t)

    return jax.shard_map(
        step,
        mesh=fine,
        in_specs=(
            P(dp, "tensor"),
            P("tensor", dp),
            P("tensor", None),
            P(None, dp),
            P("tensor"),
            P(dp, "tensor"),
        ),
        out_specs=(
            P(dp, "tensor"),
            P(("tensor",) + dp),
            P(None, ("tensor",) + dp),
            P(("tensor",) + dp, None),
        ),
        check_vma=False,
    )
```

profile of v0, /device:TPU:4, one launch (start us, length us, event | category | flops | bytes accessed | tf_op | source)
XLA Modules:
  0.0 532.2 jit_solution(16286039173848104964)
XLA Ops:
  7.2 0.0 copy-start
  7.2 0.0 copy-start.5
  7.2 0.0 copy-start.3
  7.2 0.0 all-gather.3.cloned.1.call-start
  7.2 0.7 all-gather.3.cloned.1.call-update
  7.9 1.6 collective-permute-start.1
  9.5 0.0 collective-permute-start
  9.5 144.5 %all-gather = bf16[16,288,16]{1,2,0:T(8,128)(2,1)S(1)} all-gather(bf16[1,288,16]{1,2,0:T(8,128)(2,1)} %bitcast.44), channel_id=1, replica_groups=mesh['outer'=4,'mid'=2,'core'=2,'tensor'=2] {'outer','mid','core'}, dimensions={0}, use_global_device_ids=true | all-gather | bytes 156672 | tf_op jit(solution)/shard_map/all_gather | solution.py:32
  154.0 0.2 reshape.41
  154.3 0.0 copy-done.5
  154.3 0.6 dynamic-slice
  155.5 0.0 copy-done
  155.5 0.0 copy-done.3
  155.5 0.0 copy-start.4
  155.5 0.0 copy-start.2
  155.5 4.4 fusion.3
  159.9 4.9 psum.43
  164.8 0.2 dynamic-update-slice
  165.1 80.5 %all-reduce = f32[4608]{0:T(1024)S(1)} all-reduce(f32[4608]{0:T(1024)S(1)} %dynamic-update-slice), channel_id=1, replica_groups=mesh['outer'=4,'mid'=2,'core'=2,'tensor'=2] {'outer','mid','core'}, use_global_device_ids=true, to_apply=%add | all-reduce | flops 4608 | bytes 36864
  245.6 0.0 copy-done.4
  245.6 0.1 fusion.13
  245.7 0.0 copy-done.2
  245.7 0.5 fusion.4
  246.2 4.4 fusion.18
  250.6 7.7 %all-reduce.1 = (bf16[320,16]{0,1:T(8,128)(2,1)S(1)}, bf16[320,16]{0,1:T(8,128)(2,1)S(1)}) all-reduce(f32[320,16]{0,1:T(8,128)S(1)} %fusion.4, f32[320,16]{0,1:T(8,128)S(1)} %fusion.18), channel_id=1, replica_groups=mesh['outer'=4,'mid'=2,'core'=2,'tensor'=2] {'tensor'}, use_global_device_ids=true, to_apply=%region_3.0 | all-reduce | flops 10240 | bytes 61440 | tf_op jit(solution)/shard_map/psum | solution.py:46
  258.2 0.4 fusion.6
  258.6 0.2 reshape.31
  258.8 0.2 copy.15
  259.0 3.7 fusion.19
  262.7 0.2 reshape.32
  262.9 0.2 copy.16
  263.1 1.1 maximum_bitcast_fusion
  264.2 16.8 %all-to-all-start = ((f32[16,16,720]{2,1,0:T(8,128)}), f32[16,16,720]{2,1,0:T(8,128)S(1)}, u32[]{:S(2)}, u32[]{:S(2)}) async-start(f32[16,16,720]{2,1,0:T(8,128)} %maximum_bitcast_fusion), calls=%async_computation | async-start | bytes 1572864 | tf_op jit(solution)/shard_map/all_to_all | solution.py:51
  281.0 0.0 slice-start
  281.1 0.0 slice-start.1
  281.1 0.0 collective-permute-done.1
  281.1 0.5 collective-permute-start.2
  281.5 8.7 %broadcast_in_dim.17 = bf16[4,320,9216]{2,1,0:T(8,128)(2,1)} broadcast(bf16[]{:T(256)} %constant.14.clone.1), dimensions={} | broadcast | bytes 23592962 | tf_op jit(solution)/shard_map/broadcast_in_dim | solution.py:39
  290.3 2.9 bitcast_dynamic-update-slice_fusion.3
  293.2 25.9 %all-to-all-done = f32[16,16,720]{2,1,0:T(8,128)S(1)} async-done(((f32[16,16,720]{2,1,0:T(8,128)}), f32[16,16,720]{2,1,0:T(8,128)S(1)}, u32[]{:S(2)}, u32[]{:S(2)}) %all-to-all-start) | async-done | bytes 737312 | tf_op jit(solution)/shard_map/all_to_all | solution.py:51
  319.1 0.6 slice.8
  319.7 0.7 slice_bitcast_fusion
  320.4 0.0 collective-permute-done
  320.4 5.6 %bitcast_dynamic-update-slice_fusion.2 = bf16[4,320,9216]{2,1,0:T(8,128)(2,1)} fusion(bf16[4,320,9216]{2,1,0:T(8,128)(2,1)} %bitcast_dynamic-update-slice_fusion.3, s32[]{:T(128)S(6)} %select_n.20, bf16[320,9216]{1,0:T(8,128)(2,1)} %collective-permute-done), kind=kLoop, calls=%fused_computation.6 | loop fusion | bytes 11796484 | tf_op jit(solution)/shard_map/dynamic_update_slice | solution.py:41
  326.1 5.6 %bitcast_dynamic-update-slice_fusion.1 = bf16[4,320,9216]{2,1,0:T(8,128)(2,1)} fusion(bf16[4,320,9216]{2,1,0:T(8,128)(2,1)} %bitcast_dynamic-update-slice_fusion.2, s32[]{:T(128)S(6)} %select_n.21, bf16[320,9216]{1,0:T(8,128)(2,1)} %collective-permute-done.1), kind=kLoop, calls=%fused_computation.5 | loop fusion | bytes 11796484 | tf_op jit(solution)/shard_map/dynamic_update_slice | solution.py:41
  331.6 0.0 collective-permute-done.2
  331.6 5.6 %bitcast_dynamic-update-slice_fusion = bf16[4,320,9216]{2,1,0:T(8,128)(2,1)} fusion(bf16[4,320,9216]{2,1,0:T(8,128)(2,1)} %bitcast_dynamic-update-slice_fusion.1, s32[]{:T(128)S(6)} %select_n.22, bf16[320,9216]{1,0:T(8,128)(2,1)} %collective-permute-done.2), kind=kLoop, calls=%fused_computation.4 | loop fusion | bytes 11796484 | tf_op jit(solution)/shard_map/dynamic_update_slice | solution.py:41
  337.2 52.7 %all-gather.3.cloned.1.call-done = bf16[9216,1152]{0,1:T(8,128)(2,1)} async-done(((bf16[9216,288]{0,1:T(8,128)(2,1)}), bf16[9216,1152]{0,1:T(8,128)(2,1)}) %all-gather.3.cloned.1.call-update) | async-done | bytes 21233680 | tf_op jit(solution)/shard_map/all_gather | solution.py:23
  389.9 37.6 %convolution_convert_fusion = bf16[1280,1152]{1,0:T(8,128)(2,1)} fusion(bf16[1280,9216]{1,0:T(8,128)(2,1)} %bitcast.39, bf16[9216,1152]{0,1:T(8,128)(2,1)} %all-gather.3.cloned.1.call-done), kind=kOutput, calls=%fused_computation.2 | convolution fusion | flops 27180564480 | bytes 47775744 | tf_op jit(solution)/shard_map/dot_general | solution.py:58
  427.5 3.9 copy.17
  431.5 5.1 reshape.33
  436.6 4.3 copy.18
  440.9 4.9 all-to-all-start.1
  445.8 40.7 %all-to-all-done.1 = bf16[8,2,320,288]{2,3,1,0:T(8,128)(2,1)} async-done(((bf16[8,2,320,288]{2,3,1,0:T(8,128)(2,1)}), bf16[8,2,320,288]{2,3,1,0:T(8,128)(2,1)}, u32[]{:S(2)}, u32[]{:S(2)}) %all-to-all-start.1) | async-done | bytes 2949152 | tf_op jit(solution)/shard_map/all_to_all | solution.py:61
  486.5 3.1 convert_reduce_fusion
  489.6 2.0 copy.19
  491.6 3.3 copy.20
  494.9 3.2 fusion.2
  498.2 0.1 fusion.12
  498.2 3.3 psum.45
  501.5 7.2 %psum.46 = f32[2304]{0:T(1024)S(1)} all-reduce(f32[2304]{0:T(1024)S(1)} %psum.45), channel_id=1, replica_groups=mesh['outer'=4,'mid'=2,'core'=2,'tensor'=2] {'mid'}, use_global_device_ids=true, to_apply=%region_8.0 | all-reduce | flops 2304 | bytes 18432 | tf_op jit(solution)/shard_map/psum | solution.py:69
  508.7 16.0 %psum.47 = f32[2304]{0:T(1024)S(1)} all-reduce(f32[2304]{0:T(1024)S(1)} %psum.46), channel_id=1, replica_groups=mesh['outer'=4,'mid'=2,'core'=2,'tensor'=2] {'outer'}, use_global_device_ids=true, to_apply=%region_9.0 | all-reduce | flops 2304 | bytes 18432 | tf_op jit(solution)/shard_map/psum | solution.py:69
  524.7 0.6 dynamic_slice.11
  525.4 0.0 copy-done.1
  (7 shorter events, 0.1 us)
Async XLA Ops:
  7.2 148.3 %copy-start = (bf16[9216,16]{0,1:T(8,128)(2,1)S(1)}, bf16[9216,16]{0,1:T(8,128)(2,1)}, u32[]{:S(2)}) copy-start(bf16[9216,16]{0,1:T(8,128)(2,1)} %param.8) | copy-start | bytes 884740
  7.2 147.1 %copy-start.5 = (u32[32]{0:T(128)S(1)}, u32[32]{0:T(128)}, u32[]{:S(2)}) copy-start(u32[32]{0:T(128)} %constant.38) | copy-start | bytes 388
  7.2 148.3 %copy-start.3 = (bf16[16,288]{1,0:T(8,128)(2,1)S(1)}, bf16[16,288]{1,0:T(8,128)(2,1)}, u32[]{:S(2)}) copy-start(bf16[16,288]{1,0:T(8,128)(2,1)} %param.9) | copy-start | bytes 27652
  7.2 382.7 %all-gather.3.cloned.1.call-start = ((), (), s32[]{:S(2)}) async-start(), calls=%async_computation.2 | async-start | bytes 26542080 | tf_op jit(solution)/shard_map/all_gather | solution.py:23
  7.9 273.1 %collective-permute-start.1 = (bf16[320,9216]{1,0:T(8,128)(2,1)}, bf16[320,9216]{1,0:T(8,128)(2,1)}, u32[]{:S(2)}, u32[]{:S(2)}) collective-permute-start(bf16[320,9216]{1,0:T(8,128)(2,1)} %param.6), channel_id=1, source_target_pairs={{0,4},{4,0},{1,5},{5,1},{2,6},{6,2},{3,7},{7,3},{8,12},{12,8},{9,1... | collective-permute-start | bytes 17694728 | tf_op jit(solution)/shard_map/ppermute | solution.py:22
  9.5 310.9 %collective-permute-start = (bf16[320,9216]{1,0:T(8,128)(2,1)}, bf16[320,9216]{1,0:T(8,128)(2,1)}, u32[]{:S(2)}, u32[]{:S(2)}) collective-permute-start(bf16[320,9216]{1,0:T(8,128)(2,1)} %param.6), channel_id=1, source_target_pairs={{0,2},{2,0},{1,3},{3,1},{4,6},{6,4},{5,7},{7,5},{8,10},{10,8},{9,1... | collective-permute-start | bytes 17694728 | tf_op jit(solution)/shard_map/ppermute | solution.py:24
  155.5 90.0 %copy-start.4 = (f32[2304]{0:T(1024)S(1)}, f32[2304]{0:T(1024)}, u32[]{:S(2)}) copy-start(f32[2304]{0:T(1024)} %param.10) | copy-start | bytes 27652
  155.5 90.1 %copy-start.2 = (bf16[320,2304]{1,0:T(8,128)(2,1)S(1)}, bf16[320,2304]{1,0:T(8,128)(2,1)}, u32[]{:S(2)}) copy-start(bf16[320,2304]{1,0:T(8,128)(2,1)} %param.11) | copy-start | bytes 4423684
  264.2 54.8 %all-to-all-start = ((f32[16,16,720]{2,1,0:T(8,128)}), f32[16,16,720]{2,1,0:T(8,128)S(1)}, u32[]{:S(2)}, u32[]{:S(2)}) async-start(f32[16,16,720]{2,1,0:T(8,128)} %maximum_bitcast_fusion), calls=%async_computation | async-start | bytes 1572864 | tf_op jit(solution)/shard_map/all_to_all | solution.py:51
  281.0 9.2 %slice-start = ((s8[5898240]{0:T(1024)(128)(4,1)}), s8[1703936]{0:T(1024)(128)(4,1)S(1)}, s32[]{:S(2)}) async-start(s8[5898240]{0:T(1024)(128)(4,1)} %bitcast.37), calls=%async_computation.3 | async-start | bytes 3407872
  281.1 9.2 %slice-start.1 = ((s8[5898240]{0:T(1024)(128)(4,1)}), s8[4194304]{0:T(1024)(128)(4,1)S(1)}, s32[]{:S(2)}) async-start(s8[5898240]{0:T(1024)(128)(4,1)} %bitcast.37), calls=%async_computation.4 | async-start | bytes 8388608
  281.1 50.5 %collective-permute-start.2 = (bf16[320,9216]{1,0:T(8,128)(2,1)}, bf16[320,9216]{1,0:T(8,128)(2,1)}, u32[]{:S(2)}, u32[]{:S(2)}) collective-permute-start(bf16[320,9216]{1,0:T(8,128)(2,1)} %collective-permute-done.1), channel_id=1, source_target_pairs={{0,2},{2,0},{1,3},{3,1},{4,6},{6,4},{5,7},{7,5},{8,10},{10,8},{9,1... | collective-permute-start | bytes 17694728 | tf_op jit(solution)/shard_map/ppermute | solution.py:25
  440.9 45.6 %all-to-all-start.1 = ((bf16[8,2,320,288]{2,3,1,0:T(8,128)(2,1)}), bf16[8,2,320,288]{2,3,1,0:T(8,128)(2,1)}, u32[]{:S(2)}, u32[]{:S(2)}) async-start(bf16[8,2,320,288]{2,3,1,0:T(8,128)(2,1)} %bitcast.40), calls=%async_computation.1 | async-start | bytes 7077888 | tf_op jit(solution)/shard_map/all_to_all | solution.py:61
  491.6 33.8 %copy-start.1 = (bf16[9216,16]{0,1:T(8,128)(2,1)S(1)}, bf16[9216,16]{0,1:T(8,128)(2,1)}, u32[]{:S(2)}) copy-start(bf16[9216,16]{0,1:T(8,128)(2,1)} %param.8) | copy-start | bytes 884740
Sparse Core Ops, SparseCore 0:
  9.6 380.2 all-gather.2
where the time goes:
time: 535 us; the launch traced here: 532 us
  blocking collectives  264 us (49%)
  waiting for transfers between devices  120 us (22%)
  matrix products  54.2 us (10%)
  local copies, waits for them, and re-layouts  50.8 us (9%)
  starting transfers between devices  23.8 us (4%)
  between operations  14.9 us (3%)
    all_gather x1, blocking collectives, body(): full_a = lax.all_gather(factor_a, dp, axis=1, tiled=True)  145 us
    unnamed x1, blocking collectives  80.5 us
    all_gather x1, waiting for transfers between devices, body(): w_all = lax.all_gather(weight, 'outer', axis=1, tiled=True)  52.7 us
    all_to_all x1, waiting for transfers between devices, body(): got = lax.all_to_all(sends, ('tensor', 'mid', 'core'), 0, 0, tiled=True)  40.7 us
    dot_general x1, matrix products, body(): sends = jnp.dot(h_rows, w_all, preferred_element_type=F32).astype(BF16)  37.6 us
    psum x3, blocking collectives, body(): mag_part = lax.psum(mag_part, axis)  26.5 us
    all_to_all x1, waiting for transfers between devices, body(): parts = lax.all_to_all(parts.transpose(1, 0, 2), dp, 0, 0, tiled=True)  25.9 us
    dynamic_update_slice x4, local copies, waits for them, and re-layouts, body(): h_all = lax.dynamic_update_slice_in_dim(h_all, block[None], place ^ flip, 0)  19.6 us
  transfers between devices with their start and end apart: 6, of which 3 were waited for; matrix products, arithmetic and copies ran while one was open for 9% of the time, Pallas kernels for 0%

commit v1 on v0

v1 whole, which is shorter than its diff:
```python
import functools

import jax
import jax.numpy as jnp
from jax import lax
from jax.experimental import pallas as pl
from jax.experimental.pallas import tpu as pltpu
from jax.sharding import Mesh, PartitionSpec as P

F32, BF16 = jnp.float32, jnp.bfloat16
AXES = ("u", "b", "x", "core", "tensor")
NT = (((1,), (1,)), ((), ()))
N_CHUNK = 3
H_CHUNK = 4


def split_of(size, most):
    best = 128
    for step in range(128, most + 1, 128):
        if size % step == 0:
            best = step
    return best


def bulk_kernel(
    n_u, n_x, h, w, out, hs, ws, own, part_out, part_in, scat,
    loc_sem, hc_sem, hb_sem, hr_sem, wx_sem, wa_sem, wr_sem, ps_sem, pr_sem, ss_sem, sr_sem,
):
    u, b, x, c, t = (lax.axis_index(a) for a in AXES)
    rows, depth = h.shape
    cols = w.shape[0]
    cw = cols // N_CHUNK
    hr = rows // H_CHUNK
    kc = split_of(depth, 1152)

    def at(**moved):
        here = dict(u=u, b=b, x=x, core=c, tensor=t)
        here.update(moved)
        return tuple(here[a] for a in AXES)

    def shift(value, by, n):
        return lax.rem(value + by, n)

    def far_b(k):
        return shift(b, k % 2, 2)

    core_peer = at(core=1 - c)
    b_peer = at(b=1 - b)
    diag_peer = at(b=1 - b, core=1 - c)
    x_to = [at(x=shift(x, k, n_x)) for k in range(n_x)]
    u_to = [at(u=shift(u, k, n_u), b=far_b(k)) for k in range(n_u)]
    t_to = [at(tensor=shift(t, k, n_u)) for k in range(n_u)]

    peers = [core_peer, b_peer, diag_peer] + x_to[1:] + u_to[1:] + t_to[1:]
    barrier = pltpu.get_barrier_semaphore()
    for peer in peers:
        pl.semaphore_signal(barrier, inc=1, device_id=peer, device_id_type=pl.DeviceIdType.MESH)
    pl.semaphore_wait(barrier, len(peers))

    def send(src, dst, sems, index, peer):
        return pltpu.make_async_remote_copy(
            src_ref=src,
            dst_ref=dst,
            send_sem=sems.at[(0,) + index],
            recv_sem=sems.at[(1,) + index],
            device_id=peer,
            device_id_type=pl.DeviceIdType.MESH,
        )

    def h_rows(bb, cc, i):
        return hs.at[bb, pl.ds(pl.multiple_of(cc * rows + i * hr, 16), hr), :]

    def w_rows(uu, xx, j):
        return ws.at[uu, xx, pl.ds(j * cw, cw), :]

    own_rows = hs.at[b, pl.ds(pl.multiple_of(c * rows, 16), rows), :]
    sent = []

    loads = [
        pltpu.make_async_copy(h, own_rows, loc_sem.at[0]),
        pltpu.make_async_copy(w, ws.at[u, x], loc_sem.at[1]),
    ]
    for load in loads:
        load.start()
    h_core = send(h, own_rows, hc_sem, (0,), core_peer)
    h_core.start()
    for i in range(H_CHUNK):
        copy = send(h.at[pl.ds(i * hr, hr), :], h_rows(b, c, i), hb_sem, (i,), b_peer)
        copy.start()
        sent.append(copy)
    for j in range(N_CHUNK):
        piece = w.at[pl.ds(j * cw, cw), :]
        for k in range(1, n_x):
            copy = send(piece, w_rows(u, x, j), wx_sem, (k - 1, j), x_to[k])
            copy.start()
            sent.append(copy)
        for k in range(1, n_u):
            copy = send(piece, w_rows(u, x, j), wa_sem, (k - 1, j), u_to[k])
            copy.start()
            sent.append(copy)

    def unit(bb, uu, j, take):
        def step(i, acc):
            at_k = pl.ds(pl.multiple_of(i * kc, 128), kc)
            left = hs[bb, :, at_k]
            right = jnp.concatenate([ws[uu, xx, j * cw : (j + 1) * cw, at_k] for xx in range(n_x)], axis=0)
            return acc + lax.dot_general(left, right, NT, preferred_element_type=F32)

        zero = jnp.zeros((2 * rows, n_x * cw), F32)
        take(lax.fori_loop(0, depth // kc, step, zero))

    count = [0]
    waiting = [[], []]

    def run_unit(kb, ku, j):
        place = count[0] % 2
        count[0] += 1
        bb, uu = shift(b, kb, 2), shift(u, ku, n_u)
        keep = uu == t
        slot = kb * N_CHUNK + j

        def copy():
            return send_part(slot, place, uu)

        if waiting[place]:
            old_keep, old_copy = waiting[place].pop()

            @pl.when(jnp.logical_not(old_keep))
            def _():
                old_copy().wait_send()

        def take(value):
            @pl.when(keep)
            def _():
                own[place] = value

            @pl.when(jnp.logical_not(keep))
            def _():
                part_out[place] = value.astype(BF16)
                copy().start()

        unit(bb, uu, j, take)
        waiting[place].append((keep, copy))
        return kb, uu, j, place

    def send_part(slot, place, uu):
        return pltpu.make_async_remote_copy(
            src_ref=part_out.at[place],
            dst_ref=part_in.at[slot, t],
            send_sem=ps_sem.at[place],
            recv_sem=pr_sem.at[slot, t],
            device_id=at(tensor=uu),
            device_id_type=pl.DeviceIdType.MESH,
        )

    def scatter(slot, kb, kc_, j):
        src = scat.at[slot, kc_]
        place = shift(b, (u - t + n_u), 2) * 2 + c
        index = (kb * 2 + kc_, j)
        return pltpu.make_async_remote_copy(
            src_ref=src,
            dst_ref=out.at[place, j],
            send_sem=ss_sem.at[index],
            recv_sem=sr_sem.at[index],
            device_id=at(b=shift(b, kb, 2), core=shift(c, kc_, 2)),
            device_id_type=pl.DeviceIdType.MESH,
        )

    def finish(kb, uu, j, place):
        slot = kb * N_CHUNK + j

        @pl.when(uu == t)
        def _():
            for k in range(1, n_u):
                frm = shift(t, k, n_u)
                pltpu.make_async_remote_copy(
                    src_ref=part_out.at[0],
                    dst_ref=part_in.at[slot, frm],
                    send_sem=ps_sem.at[0],
                    recv_sem=pr_sem.at[slot, frm],
                    device_id=t_to[k],
                    device_id_type=pl.DeviceIdType.MESH,
                ).wait_recv()
            for kc_ in range(2):
                at_c = pl.ds(pl.multiple_of(shift(c, kc_, 2) * rows, 16), rows)
                total = own[place, at_c, :]
                for k in range(1, n_u):
                    total = total + part_in[slot, shift(t, k, n_u), at_c, :].astype(F32)
                if kb == 0 and kc_ == 0:
                    out[shift(b, (u - t + n_u), 2) * 2 + c, j] = total.astype(BF16)
                else:
                    scat[slot, kc_] = total.astype(BF16)
                    scatter(slot, kb, kc_, j).start()

    pending = []

    def go(kb, ku, j):
        new = run_unit(kb, ku, j)
        if pending:
            finish(*pending.pop())
        pending.append(new)

    for load in loads:
        load.wait()
    h_core_in = hs.at[b, pl.ds(pl.multiple_of((1 - c) * rows, 16), rows), :]
    send(h, h_core_in, hc_sem, (0,), core_peer).wait_recv()
    relays = []

    def pass_h(i):
        got = h_rows(1 - b, c, i)
        send(got, got, hb_sem, (i,), b_peer).wait_recv()
        relay = send(got, got, hr_sem, (i,), core_peer)
        relay.start()
        relays.append(relay)

    passed = 0
    for j in range(N_CHUNK):
        while passed < H_CHUNK * (j + 1) // N_CHUNK:
            pass_h(passed)
            passed += 1
        for k in range(1, n_x):
            frm = shift(x, n_x - k, n_x)
            send(w_rows(u, frm, j), w_rows(u, frm, j), wx_sem, (k - 1, j), x_to[k]).wait_recv()
        go(0, 0, j)
    for i in range(H_CHUNK):
        got = h_rows(1 - b, 1 - c, i)
        send(got, got, hr_sem, (i,), core_peer).wait_recv()
    for j in range(N_CHUNK):
        go(1, 0, j)

    for k in range(1, n_u):
        frm_u = shift(u, n_u - k, n_u)

        def pass_w(j):
            got = w_rows(frm_u, x, j)
            send(got, got, wa_sem, (k - 1, j), u_to[k]).wait_recv()
            for m in range(1, n_x):
                relay = send(got, got, wr_sem, (k - 1, m - 1, j), x_to[m])
                relay.start()
                relays.append(relay)

        pass_w(0)
        for j in range(N_CHUNK):
            if j + 1 < N_CHUNK:
                pass_w(j + 1)
            for m in range(1, n_x):
                got = w_rows(frm_u, shift(x, n_x - m, n_x), j)
                send(got, got, wr_sem, (k - 1, m - 1, j), x_to[m]).wait_recv()
            for kb in range(2):
                go(kb, n_u - k, j)
    finish(*pending.pop())

    for place in range(2):
        for keep, copy in waiting[place]:

            @pl.when(jnp.logical_not(keep))
            def _():
                copy().wait_send()

    for copy in sent + relays + [h_core]:
        copy.wait_send()
    for kb in range(2):
        for kc_ in range(2):
            if kb or kc_:
                for j in range(N_CHUNK):
                    scatter(kb * N_CHUNK + j, kb, kc_, j).wait_send()
                    frm = shift(shift(b, kb, 2), (u - t + n_u), 2) * 2 + shift(c, kc_, 2)
                    index = (kb * 2 + kc_, j)
                    pltpu.make_async_remote_copy(
                        src_ref=out.at[frm, j],
                        dst_ref=out.at[frm, j],
                        send_sem=ss_sem.at[index],
                        recv_sem=sr_sem.at[index],
                        device_id=core_peer,
                        device_id_type=pl.DeviceIdType.MESH,
                    ).wait_recv()


def bulk(hidden, weight_t, n_u, n_x):
    rows, depth = hidden.shape
    cols = weight_t.shape[0]
    cw = cols // N_CHUNK
    wide = n_x * cw
    dma = pltpu.SemaphoreType.DMA
    few = max(n_x - 1, 1)
    return pl.pallas_call(
        functools.partial(bulk_kernel, n_u, n_x),
        out_shape=jax.ShapeDtypeStruct((4, N_CHUNK, rows, wide), BF16),
        in_specs=[pl.BlockSpec(memory_space=pltpu.HBM)] * 2,
        out_specs=pl.BlockSpec(memory_space=pltpu.VMEM),
        scratch_shapes=[
            pltpu.VMEM((2, 2 * rows, depth), BF16),
            pltpu.VMEM((n_u, n_x, cols, depth), BF16),
            pltpu.VMEM((2, 2 * rows, wide), F32),
            pltpu.VMEM((2, 2 * rows, wide), BF16),
            pltpu.VMEM((2 * N_CHUNK, n_u, 2 * rows, wide), BF16),
            pltpu.VMEM((2 * N_CHUNK, 2, rows, wide), BF16),
            dma((2,)),
            dma((2, 1)),
            dma((2, H_CHUNK)),
            dma((2, H_CHUNK)),
            dma((2, few, N_CHUNK)),
            dma((2, n_u - 1, N_CHUNK)),
            dma((2, n_u - 1, few, N_CHUNK)),
            dma((2,)),
            dma((2 * N_CHUNK, n_u)),
            dma((4, N_CHUNK)),
            dma((4, N_CHUNK)),
        ],
        compiler_params=pltpu.CompilerParams(
            collective_id=0, has_side_effects=True, vmem_limit_bytes=67043328
        ),
        name="bulk",
    )(hidden, weight_t)


def body(hidden, weight, factor_b, factor_a, magnitude, cotangent, *, n_u, n_x):
    rows, depth = hidden.shape
    cols = weight.shape[1]
    rank = factor_b.shape[1]
    out_cols = magnitude.shape[0]
    dp = ("u", "b", "x", "core")
    n_dp = n_u * 2 * n_x * 2
    own = lax.axis_index("tensor")

    low_part = jnp.dot(hidden, factor_b, preferred_element_type=F32)
    merged = weight.astype(F32) + jnp.dot(factor_b, factor_a, preferred_element_type=F32)
    local_sq = jnp.sum(merged * merged, axis=0)
    low, block_sq = lax.psum((low_part, local_sq), "tensor")
    col_sq = lax.all_gather(block_sq, dp, axis=0, tiled=True)
    full_a = lax.all_gather(factor_a, dp, axis=1, tiled=True)
    norms = jnp.sqrt(lax.dynamic_slice_in_dim(col_sq, own * out_cols, out_cols, 0) + 1e-06)
    scale = magnitude / norms
    low_b = low.astype(BF16)
    own_a = lax.dynamic_slice_in_dim(full_a, own * out_cols, out_cols, 1)
    adapter = jnp.dot(low_b, own_a, preferred_element_type=F32)

    cot = cotangent.astype(F32)
    dpre_b = (cot * scale).astype(BF16)
    back_b = lax.psum(jnp.dot(dpre_b, own_a.T, preferred_element_type=F32), "tensor").astype(BF16)
    b_part = jnp.dot(back_b.T, hidden, preferred_element_type=F32)
    a_part = jnp.dot(low_b.T, dpre_b, preferred_element_type=F32)
    parts = jnp.concatenate([v.reshape(rank, n_dp, -1) for v in (a_part, b_part)], axis=2)
    parts = lax.all_to_all(parts.transpose(1, 0, 2), dp, 0, 0, tiled=True)
    sums = jnp.sum(parts, axis=0)
    grad_a = sums[:, : out_cols // n_dp]
    grad_b = sums[:, out_cols // n_dp :].T

    got = bulk(hidden, weight.T, n_u, n_x)
    cw = cols // N_CHUNK
    got = got.reshape(2, 2, N_CHUNK, rows, n_x, cw).transpose(3, 0, 4, 1, 2, 5).reshape(rows, out_cols)
    pre = got.astype(F32) + adapter
    mixed = (pre * scale).astype(BF16)
    mag_part = jnp.sum(cot * pre, axis=0) / norms
    mag_part = lax.psum(mag_part, dp)
    me = lax.axis_index(dp)
    grad_scale = lax.dynamic_slice_in_dim(mag_part, me * (out_cols // n_dp), out_cols // n_dp, 0)
    return mixed, grad_scale, grad_a, grad_b


def solution(mesh):
    n_dp, n_u = mesh.shape["dp"], mesh.shape["tensor"]
    n_x = n_dp // (4 * n_u)
    fine = Mesh(mesh.devices.reshape(n_u, 2, n_x, 2, n_u), AXES)
    dp = ("u", "b", "x", "core")

    def step(*args):
        return body(*args, n_u=n_u, n_x=n_x)

    return jax.shard_map(
        step,
        mesh=fine,
        in_specs=(
            P(dp, "tensor"),
            P("tensor", dp),
            P("tensor", None),
            P(None, dp),
            P("tensor"),
            P(dp, "tensor"),
        ),
        out_specs=(
            P(dp, "tensor"),
            P(("tensor",) + dp),
            P(None, ("tensor",) + dp),
            P(("tensor",) + dp, None),
        ),
        check_vma=False,
    )
```

time: 535 us -> 609 us (1.14)
  Pallas kernels: 0 us -> 326 us
  waiting for transfers between devices: 120 us -> 0.01 us
  local copies, waits for them, and re-layouts: 50.8 us -> 13.3 us
  matrix products: 54.2 us -> 17.6 us
  blocking collectives: 264 us -> 236 us
  starting transfers between devices: 23.8 us -> 4.28 us
  between operations: 14.9 us -> 1.5 us
    pallas_call x0 -> x1, Pallas kernels: none -> 326 us  [bulk(): pl.pallas_call(functools.partial(bulk_kernel, n_u, n_x), out_shape=jax.Sh...]
    all_gather x1, blocking collectives: 145 us -> 17.7 us  [body(): full_a = lax.all_gather(factor_a, dp, axis=1, tiled=True)]
    psum x4 -> x1, blocking collectives: 34.2 us -> 145 us  [body(): mag_part = lax.psum(mag_part, dp)]
    all_gather x1 -> x0, waiting for transfers between devices: 52.7 us -> none  [body(): w_all = lax.all_gather(weight, 'outer', axis=1, tiled=True)]
    all_to_all x1 -> x0, waiting for transfers between devices: 40.7 us -> none  [body(): got = lax.all_to_all(sends, ('tensor', 'mid', 'core'), 0, 0, tiled=True)]
    dot_general x1 -> x0, matrix products: 37.6 us -> none  [body(): sends = jnp.dot(h_rows, w_all, preferred_element_type=F32).astype(BF16)]
    all_to_all x1, waiting for transfers between devices: 25.9 us -> 0.01 us  [body(): parts = lax.all_to_all(parts.transpose(1, 0, 2), dp, 0, 0, tiled=True)]
    unnamed x1, blocking collectives: 80.5 us -> 60.3 us
  transfers between devices with their start and end apart: 6 -> 1, of which waited for: 3 -> 0; matrix products, arithmetic and copies ran while one was open for 9% -> 2% of each run, Pallas kernels for 0% -> 54%
where the time goes in v1:
time: 609 us; the launch traced here: 601 us
  Pallas kernels  326 us (54%)
  blocking collectives  236 us (39%)
  matrix products  17.6 us (3%)
  local copies, waits for them, and re-layouts  13.3 us (2%)
    pallas_call x1, Pallas kernels, bulk(): pl.pallas_call(functools.partial(bulk_kernel, n_u, n_x), out_shape=jax.Sh...  326 us
    psum x1, blocking collectives, body(): mag_part = lax.psum(mag_part, dp)  145 us
    unnamed x1, blocking collectives  60.3 us
    all_gather x1, blocking collectives, body(): full_a = lax.all_gather(factor_a, dp, axis=1, tiled=True)  17.7 us
    psum x2, blocking collectives, body(): low, block_sq = lax.psum((low_part, local_sq), 'tensor')  12.6 us
  transfers between devices with their start and end apart: 1, of which 0 were waited for; matrix products, arithmetic and copies ran while one was open for 2% of the time, Pallas kernels for 54%

profile of v1, /device:TPU:4, one launch (start us, length us, event | category | flops | bytes accessed | tf_op | source)
XLA Modules:
  0.0 601.2 jit_solution(6923478402689443891)
XLA Ops:
  0.6 0.0 copy-start.10
  0.7 0.0 copy-start.2
  0.7 4.4 fusion.3
  5.1 4.9 psum.29
  10.0 0.0 copy-done.10
  10.0 0.6 dynamic-slice
  11.2 0.3 dynamic-update-slice
  11.5 60.3 %all-reduce = f32[4608]{0:T(1024)S(1)} all-reduce(f32[4608]{0:T(1024)S(1)} %dynamic-update-slice), channel_id=1, replica_groups=mesh['u'=2,'b'=2,'x'=2,'core'=2,'tensor'=2] {'u','b','x','core'}, use_global_device_ids=true, to_apply=%add | all-reduce | flops 4608 | bytes 36864
  71.8 0.0 copy-start.5
  71.8 0.0 copy-done.2
  71.8 0.0 copy-start.8
  71.8 0.0 copy-start.9
  71.8 0.0 copy-start
  71.8 4.4 fusion.18
  76.3 0.0 copy-done.8
  76.3 17.7 %all-gather = bf16[16,288,16]{1,2,0:T(8,128)(2,1)S(1)} all-gather(bf16[1,288,16]{1,2,0:T(8,128)(2,1)S(1)} %bitcast.26), channel_id=1, replica_groups=mesh['u'=2,'b'=2,'x'=2,'core'=2,'tensor'=2] {'u','b','x','core'}, dimensions={0}, use_global_device_ids=true | all-gather | bytes 156672 | tf_op jit(solution)/shard_map/all_gather | solution.py:331
  94.0 0.2 reshape.29
  94.2 0.0 copy-start.1
  94.2 0.0 copy-done.5
  94.2 0.0 copy-done.9
  94.2 0.1 fusion.13
  94.3 0.0 copy-done
  94.3 0.0 copy-start.3
  94.3 0.5 fusion.4
  94.9 7.6 %all-reduce.1 = (bf16[320,16]{0,1:T(8,128)(2,1)S(1)}, bf16[320,16]{0,1:T(8,128)(2,1)S(1)}) all-reduce(f32[320,16]{0,1:T(8,128)S(1)} %fusion.18, f32[320,16]{0,1:T(8,128)S(1)} %fusion.4), channel_id=1, replica_groups=mesh['u'=2,'b'=2,'x'=2,'core'=2,'tensor'=2] {'tensor'}, use_global_device_ids=true, to_apply=%region_0.0 | all-reduce | flops 10240 | bytes 61440 | tf_op jit(solution)/shard_map/psum | solution.py:329
  102.5 0.0 copy-done.1
  102.5 0.0 copy-start.7
  102.5 3.7 fusion.19
  106.2 0.2 reshape.22
  106.4 0.2 copy.26
  106.6 0.0 copy-done.3
  106.6 0.0 copy-done.7
  106.6 0.4 fusion.6
  107.0 0.2 reshape.21
  107.2 0.2 copy.25
  107.4 1.1 maximum_bitcast_fusion
  108.5 4.3 all-to-all-start
  112.8 326.1 %bulk.1 = bf16[4,3,320,192]{3,2,1,0:T(8,128)(2,1)} custom-call(bf16[320,9216]{1,0:T(8,128)(2,1)} %h.1, bf16[288,9216]{1,0:T(8,128)(2,1)} %bitcast.25), custom_call_target="tpu_custom_call" | custom-call | tf_op jit(solution)/shard_map/bulk/pallas_call | solution.py:286
  438.9 4.2 copy.21
  443.2 2.2 copy.22
  445.4 0.0 copy-start.4
  445.4 3.0 copy.24
  448.4 0.0 copy-done.4
  448.4 0.0 copy-start.6
  448.4 4.2 fusion.1
  452.6 0.0 copy-done.6
  452.6 0.1 fusion.12
  452.7 145.4 %psum.30 = f32[2304]{0:T(1024)S(1)} all-reduce(f32[2304]{0:T(1024)S(1)} %fusion.12), channel_id=1, replica_groups=mesh['u'=2,'b'=2,'x'=2,'core'=2,'tensor'=2] {'u','b','x','core'}, use_global_device_ids=true, to_apply=%region_4.0 | all-reduce | flops 2304 | bytes 18432 | tf_op jit(solution)/shard_map/psum | solution.py:355
  598.1 0.6 dynamic_slice.11
  598.7 0.0 all-to-all-done
  598.7 1.2 reduce_sum.29
  599.9 0.6 slice.8
  600.5 0.7 slice_bitcast_fusion
  (2 shorter events, 0.0 us)
Async XLA Ops:
  0.6 9.4 %copy-start.10 = (u32[32]{0:T(128)S(1)}, u32[32]{0:T(128)}, u32[]{:S(2)}) copy-start(u32[32]{0:T(128)} %constant.38) | copy-start | bytes 388
  0.7 71.2 %copy-start.2 = (bf16[9216,16]{0,1:T(8,128)(2,1)S(1)}, bf16[9216,16]{0,1:T(8,128)(2,1)}, u32[]{:S(2)}) copy-start(bf16[9216,16]{0,1:T(8,128)(2,1)} %param.8) | copy-start | bytes 884740
  71.8 22.4 %copy-start.5 = (f32[4608]{0:T(1024)}, f32[4608]{0:T(1024)S(1)}, u32[]{:S(2)}) copy-start(f32[4608]{0:T(1024)S(1)} %all-reduce) | copy-start | bytes 55300
  71.8 4.4 copy-start.8
  71.8 22.4 %copy-start.9 = (f32[2304]{0:T(1024)S(1)}, f32[2304]{0:T(1024)}, u32[]{:S(2)}) copy-start(f32[2304]{0:T(1024)} %param.10) | copy-start | bytes 27652
  71.8 22.5 %copy-start = (bf16[320,2304]{1,0:T(8,128)(2,1)S(1)}, bf16[320,2304]{1,0:T(8,128)(2,1)}, u32[]{:S(2)}) copy-start(bf16[320,2304]{1,0:T(8,128)(2,1)} %param.11) | copy-start | bytes 4423684
  94.2 8.3 %copy-start.1 = (bf16[4608,16]{0,1:T(8,128)(2,1)}, bf16[4608,16]{0,1:T(8,128)(2,1)S(1)}, u32[]{:S(2)}) copy-start(bf16[4608,16]{0,1:T(8,128)(2,1)S(1)} %reshape.29) | copy-start | bytes 442372
  94.3 12.3 %copy-start.3 = (f32[2304]{0:T(1024)}, f32[2304]{0:T(1024)S(1)}, u32[]{:S(2)}) copy-start(f32[2304]{0:T(1024)S(1)} %fusion.13) | copy-start | bytes 27652
  102.5 4.2 copy-start.7
  108.5 490.2 %all-to-all-start = ((f32[16,16,720]{2,1,0:T(8,128)}), f32[16,16,720]{2,1,0:T(8,128)}, u32[]{:S(2)}, u32[]{:S(2)}) async-start(f32[16,16,720]{2,1,0:T(8,128)} %maximum_bitcast_fusion), calls=%async_computation | async-start | bytes 1572864 | tf_op jit(solution)/shard_map/all_to_all | solution.py:344
  445.4 3.0 copy-start.4
  448.4 4.2 copy-start.6

commit v2 on v0

v2 whole, which is shorter than its diff:
```python
import functools

import jax
import jax.numpy as jnp
from jax import lax
from jax.experimental import pallas as pl
from jax.experimental.pallas import tpu as pltpu
from jax.sharding import Mesh, PartitionSpec as P

F32, BF16 = jnp.float32, jnp.bfloat16
AXES = ("u", "b", "x", "core", "tensor")
MESH = pl.DeviceIdType.MESH
NT = (((1,), (1,)), ((), ()))
NN = (((1,), (0,)), ((), ()))
TN = (((0,), (0,)), ((), ()))
H_CHUNK = 4
PIECE = 64
LANES = 128


def split_of(size, most):
    best = LANES
    for step in range(LANES, most + 1, LANES):
        if size % step == 0:
            best = step
    return best


def cuts(size, step):
    return [(at, min(step, size - at)) for at in range(0, size, step)]


def granule(depth, n_dp):
    share = depth // n_dp
    size = share
    while size % LANES:
        size += share
    return size


def dot(left, right, dims):
    return lax.dot_general(left, right, dims, preferred_element_type=F32)


def kernel(
    n_u, n_x, h, w, bt, a, mag, cot, mixed, mag_out, ga_out, gb_out,
    hs, ws, own, part_out, part_in, scat, got_out, sq, sqx, low, lowx, back, backx, backs, pk, pks,
    ga, gax, gb, gbx, mg, mgx,
    loc_sem, hc_sem, hb_sem, hr_sem, wx_sem, wa_sem, wr_sem, ps_sem, pr_sem, sc_sem,
    sq_sem, low_sem, back_sem, tok_sem, pk_ssem, pk_rsem, ga_sem, gb_sem, mg_sem,
):
    u, b, x, c, t = (lax.axis_index(name) for name in AXES)
    rows, depth = h.shape
    cols = w.shape[0]
    rank = a.shape[0]
    n_blk = 4 * n_x
    n_dp = n_blk * n_u
    hr = rows // H_CHUNK
    kc = split_of(depth, 1152)
    chunks = cuts(cols, LANES)
    pieces = cuts(cols, PIECE)
    n_ch, n_pc = len(chunks), len(pieces)

    def at(**moved):
        here = dict(u=u, b=b, x=x, core=c, tensor=t)
        here.update(moved)
        return tuple(here[name] for name in AXES)

    def shift(value, by, n):
        return lax.rem(value + by, n)

    def remote(src, dst, send_sem, recv_sem, peer):
        return pltpu.make_async_remote_copy(
            src_ref=src, dst_ref=dst, send_sem=send_sem, recv_sem=recv_sem, device_id=peer, device_id_type=MESH
        )

    def send(src, dst, sems, index, peer):
        return remote(src, dst, sems.at[(0,) + index], sems.at[(1,) + index], peer)

    core_peer = at(core=1 - c)
    b_peer = at(b=1 - b)
    x_to = [at(x=shift(x, k, n_x)) for k in range(n_x)]
    u_to = [at(u=shift(u, k, n_u), b=shift(b, k % 2, 2)) for k in range(n_u)]
    t_to = [at(tensor=shift(t, k, n_u)) for k in range(n_u)]
    steps = [(i, j, k, l) for i in range(n_u) for j in range(2) for k in range(n_x) for l in range(2)]

    def moved(step):
        du, db, dx, dc = step
        return at(u=shift(u, du, n_u), b=shift(b, db, 2), x=shift(x, dx, n_x), core=shift(c, dc, 2))

    def place_of(device):
        return ((device[0] * 2 + device[1]) * n_x + device[2]) * 2 + device[3]

    def block_of(bb, xx, cc):
        return (bb * n_x + xx) * 2 + cc

    far = shift(b, u - t + n_u, 2)

    peers = [moved(step) for step in steps[1:]] + t_to[1:]
    barrier = pltpu.get_barrier_semaphore()
    for peer in peers:
        pl.semaphore_signal(barrier, inc=1, device_id=peer, device_id_type=MESH)
    pl.semaphore_wait(barrier, len(peers))

    def h_rows(bb, cc, i):
        return hs.at[bb, pl.ds(pl.multiple_of(cc * rows + i * hr, 16), hr), :]

    def w_rows(uu, xx, p):
        first, size = pieces[p]
        return ws.at[uu, xx, pl.ds(first, size), :]

    own_rows = hs.at[b, pl.ds(pl.multiple_of(c * rows, 16), rows), :]
    sent = []

    def start(copy):
        copy.start()
        sent.append(copy)

    def start_h(i):
        start(send(h.at[pl.ds(i * hr, hr), :], h_rows(b, c, i), hb_sem, (i,), b_peer))

    def start_wx(p):
        first, size = pieces[p]
        for k in range(1, n_x):
            start(send(w.at[pl.ds(first, size), :], w_rows(u, x, p), wx_sem, (k - 1, p), x_to[k]))

    def wa(k, p):
        first, size = pieces[p]
        return send(w.at[pl.ds(first, size), :], w_rows(u, x, p), wa_sem, (k - 1, p), u_to[k])

    def start_wa(p):
        for k in range(1, n_u):
            wa(k, p).start()

    early = u != b

    loads = [
        pltpu.make_async_copy(w, ws.at[u, x], loc_sem.at[1]),
        pltpu.make_async_copy(h, own_rows, loc_sem.at[0]),
    ]
    for load in loads:
        load.start()
    start(send(h, own_rows, hc_sem, (0,), core_peer))
    start_h(0)
    start_wx(0)

    @pl.when(early)
    def _():
        start_wa(0)

    loads[0].wait()
    a_t = jnp.transpose(a[...].astype(F32)).astype(BF16)

    def square_step(i, acc):
        at_k = pl.ds(pl.multiple_of(i * kc, LANES), kc)
        merged = ws[u, x, :, at_k].astype(F32) + dot(a_t, bt[:, at_k], NN)
        for g in range(kc // LANES):
            part = merged[:, g * LANES : (g + 1) * LANES]
            acc = acc + part * part
        return acc

    squares = lax.fori_loop(0, depth // kc, square_step, jnp.zeros((cols, LANES), F32))
    sq[...] = lax.dot_general(
        jnp.ones((8, LANES), F32), squares, NT, precision=lax.Precision.HIGHEST, preferred_element_type=F32
    )
    for k in range(1, n_u):
        start(send(sq, sqx.at[k - 1], sq_sem, (k - 1,), t_to[k]))

    loads[1].wait()

    def low_step(i, acc):
        at_k = pl.ds(pl.multiple_of(i * kc, LANES), kc)
        left = hs[b, pl.ds(pl.multiple_of(c * rows, 16), rows), at_k]
        return acc + dot(bt[:, at_k], left, NT)

    low[...] = lax.fori_loop(0, depth // kc, low_step, jnp.zeros((rank, rows), F32))
    for k in range(1, n_u):
        start(send(low, lowx.at[k - 1], low_sem, (k - 1,), t_to[k]))

    def from_t(ref, extra, sems):
        total = ref[...]
        for k in range(1, n_u):
            send(ref, extra.at[k - 1], sems, (k - 1,), t_to[k]).wait_recv()
            total = total + extra[k - 1]
        return total

    square_sum = from_t(sq, sqx, sq_sem)
    mine = block_of(b, x, c)

    def packet(n, step):
        return remote(
            pks, pk.at[mine], pk_ssem.at[n], pk_rsem.at[n % n_blk], moved(step)
        )

    @pl.when(u == t)
    def _():
        pks[0:rank, :] = a[...].astype(F32)
        pks[rank : rank + 8, :] = square_sum
        pk[mine, 0:rank, :] = a[...].astype(F32)
        pk[mine, rank : rank + 8, :] = square_sum
        for n, step in enumerate(steps):
            if n:
                packet(n, step).start()

    start_h(1)
    start_wx(1)

    @pl.when(early)
    def _():
        start_wa(1)

    low_t = from_t(low, lowx, low_sem)
    low_tb = low_t.astype(BF16)
    low_b = jnp.transpose(low_t).astype(BF16)

    count = [0]
    waiting = [[], []]

    def run_unit(kb, ku, j):
        first, size = chunks[j]
        wide = n_x * size
        place = count[0] % 2
        count[0] += 1
        bb, uu = shift(b, kb, 2), shift(u, ku, n_u)
        keep = uu == t
        slot = kb * n_ch + j

        def copy():
            lag = lax.rem(uu - t + n_u - 1 + n_u, n_u)
            return remote(
                part_out.at[place], part_in.at[slot, lag], ps_sem.at[place], pr_sem.at[slot, lag], at(tensor=uu)
            )

        if waiting[place]:
            old_keep, old_copy = waiting[place].pop()

            @pl.when(jnp.logical_not(old_keep))
            def _():
                old_copy().wait_send()

        own[place, :, 0:wide] = jnp.zeros((2 * rows, wide), F32)

        def unit_step(i, carry):
            at_k = pl.ds(pl.multiple_of(i * kc, LANES), kc)
            right = jnp.concatenate([ws[uu, xx, first : first + size, at_k] for xx in range(n_x)], axis=0)
            own[place, :, 0:wide] += dot(hs[bb, :, at_k], right, NT)
            return carry

        lax.fori_loop(0, depth // kc, unit_step, 0)

        @pl.when(jnp.logical_not(keep))
        def _():
            part_out[place, :, 0:wide] = own[place, :, 0:wide].astype(BF16)
            copy().start()

        waiting[place].append((keep, copy))
        return kb, uu, j, place

    def scatter(kb, kc_, j):
        index = (kb * 2 + kc_, j)
        return send(
            scat.at[kb * n_ch + j, kc_], got_out.at[far * 2 + c, j], sc_sem, index,
            at(b=shift(b, kb, 2), core=shift(c, kc_, 2)),
        )

    def finish(kb, uu, j, place):
        slot = kb * n_ch + j
        wide = n_x * chunks[j][1]

        @pl.when(uu == t)
        def _():
            for k in range(n_u - 1):
                remote(part_out.at[0], part_in.at[slot, k], ps_sem.at[0], pr_sem.at[slot, k], t_to[1]).wait_recv()
            for kc_ in range(2):
                at_c = pl.ds(pl.multiple_of(shift(c, kc_, 2) * rows, 16), rows)
                total = own[place, at_c, 0:wide]
                for k in range(n_u - 1):
                    total = total + part_in[slot, k, at_c, 0:wide].astype(F32)
                if kb == 0 and kc_ == 0:
                    got_out[far * 2 + c, j, :, 0:wide] = total.astype(BF16)
                else:
                    scat[slot, kc_, :, 0:wide] = total.astype(BF16)
                    scatter(kb, kc_, j).start()

    pending = []

    def go(kb, ku, j):
        new = run_unit(kb, ku, j)
        if pending:
            finish(*pending.pop())
        pending.append(new)

    passed = [0]

    def pass_h():
        i = passed[0]
        passed[0] += 1
        got = h_rows(1 - b, c, i)
        send(got, got, hb_sem, (i,), b_peer).wait_recv()
        start(send(got, got, hr_sem, (i,), core_peer))

    def near(p):
        for k in range(1, n_x):
            got = w_rows(u, shift(x, n_x - k, n_x), p)
            send(got, got, wx_sem, (k - 1, p), x_to[k]).wait_recv()

    def of_chunk(j):
        first, size = chunks[j]
        return [p for p in range(n_pc) if first <= pieces[p][0] < first + size]

    for q in range(n_blk):
        _, db, dx, dc = steps[q]
        src = block_of(shift(b, db, 2), shift(x, n_x - dx, n_x), shift(c, dc, 2))
        wait = remote(pks, pk.at[src], pk_ssem.at[0], pk_rsem.at[q], core_peer)
        if q:
            wait.wait_recv()
        else:
            pl.when(u != t)(wait.wait_recv)

    def scale_of(i, first, size):
        norm = jnp.sqrt(pk[i, rank : rank + 1, first : first + size] + 1e-06)
        return mag[:, i * cols + first : i * cols + first + size] / norm

    back_part = jnp.zeros((rank, rows), F32)
    for i in range(n_blk):
        piece = cot[:, i * cols : (i + 1) * cols].astype(F32)
        dpre = (piece * scale_of(i, 0, cols)).astype(BF16)
        back_part = back_part + dot(pk[i, 0:rank, :].astype(BF16), dpre, NT)
        ga[i] = dot(low_tb, dpre, NN).astype(BF16)
    back[...] = back_part
    for k in range(1, n_u):
        start(send(back, backx.at[k - 1], back_sem, (k - 1,), t_to[k]))
    for n, step in enumerate(steps):
        if n:
            peer = moved(step)
            start(send(ga.at[lax.div(place_of(peer), n_u)], gax.at[n], ga_sem, (n,), peer))
    back_b = from_t(back, backx, back_sem).astype(BF16)
    backs[b * 2 + c] = back_b
    for k in range(1, 4):
        peer = at(b=shift(b, k // 2, 2), core=shift(c, k % 2, 2))
        start(send(backs.at[b * 2 + c], backs.at[b * 2 + c], tok_sem, (k - 1,), peer))

    for i in range(2, H_CHUNK):
        start_h(i)
    for p in range(2, n_pc):
        start_wx(p)

    @pl.when(early)
    def _():
        for p in range(2, n_pc):
            start_wa(p)

    @pl.when(jnp.logical_not(early))
    def _():
        for p in range(2):
            start_wa(p)

    h_core_in = hs.at[b, pl.ds(pl.multiple_of((1 - c) * rows, 16), rows), :]
    send(h, h_core_in, hc_sem, (0,), core_peer).wait_recv()
    for j in range(n_ch):
        while passed[0] < H_CHUNK * (j + 1) // n_ch:
            pass_h()
        for p in of_chunk(j):
            near(p)
        go(0, 0, j)
    for i in range(H_CHUNK):
        got = h_rows(1 - b, 1 - c, i)
        send(got, got, hr_sem, (i,), core_peer).wait_recv()

    for k in range(1, 4):
        src = shift(b, k // 2, 2) * 2 + shift(c, k % 2, 2)
        send(backs.at[src], backs.at[src], tok_sem, (k - 1,), core_peer).wait_recv()

    def grad_step(i, carry):
        at_k = pl.ds(pl.multiple_of(i * kc, LANES), kc)
        total = jnp.zeros((rank, kc), F32)
        for bb in range(2):
            for cc in range(2):
                total = total + dot(backs[bb * 2 + cc], hs[bb, cc * rows : (cc + 1) * rows, at_k], NN)
        gb[:, at_k] = total
        return carry

    lax.fori_loop(0, depth // kc, grad_step, 0)
    size_b = granule(depth, n_dp)
    share_b = depth // n_dp

    def lanes_of(device):
        return pl.ds(pl.multiple_of(lax.div(place_of(device) * share_b, size_b) * size_b, LANES), size_b)

    groups = [step for step in steps if step[1] == 0 and step[3] == 0]
    for n, step in enumerate(groups):
        if n:
            peer = moved(step)
            start(send(gb.at[:, lanes_of(peer)], gbx.at[n], gb_sem, (n,), peer))

    @pl.when(jnp.logical_not(early))
    def _():
        for p in range(2, n_pc):
            start_wa(p)

    for j in range(n_ch):
        go(1, 0, j)

    for k in range(1, n_u):
        frm_u = shift(u, n_u - k, n_u)

        def pass_w(j):
            for p in of_chunk(j):
                got = w_rows(frm_u, x, p)
                send(got, got, wa_sem, (k - 1, p), u_to[k]).wait_recv()
                for m in range(1, n_x):
                    start(send(got, got, wr_sem, (k - 1, m - 1, p), x_to[m]))

        pass_w(0)
        for j in range(n_ch):
            if j + 1 < n_ch:
                pass_w(j + 1)
            for p in of_chunk(j):
                for m in range(1, n_x):
                    got = w_rows(frm_u, shift(x, n_x - m, n_x), p)
                    send(got, got, wr_sem, (k - 1, m - 1, p), x_to[m]).wait_recv()
            for kb in range(2):
                go(kb, n_u - k, j)
    finish(*pending.pop())

    for bb in range(2):
        for cc in range(2):
            for j, (first, size) in enumerate(chunks):
                slot = bb * 2 + cc

                @pl.when(jnp.logical_or(bb != far, cc != c))
                def _():
                    kind = lax.rem(bb + far, 2) * 2 + lax.rem(cc + c, 2)
                    got = got_out.at[slot, j]
                    send(got, got, sc_sem, (kind, j), core_peer).wait_recv()

                for xx in range(n_x):
                    i = block_of(bb, xx, cc)
                    left = i * cols + first
                    pre = got_out[slot, j, :, xx * size : (xx + 1) * size].astype(F32)
                    pre = pre + dot(low_b, pk[i, 0:rank, first : first + size].astype(BF16), NN)
                    mixed[:, left : left + size] = (pre * scale_of(i, first, size)).astype(BF16)
                    part = jnp.sum(cot[:, left : left + size].astype(F32) * pre, axis=0, keepdims=True)
                    mg[i, 0:1, first : first + size] = part
    for n, step in enumerate(steps):
        if n:
            peer = moved(step)
            start(send(mg.at[lax.div(place_of(peer), n_u)], mgx.at[n], mg_sem, (n,), peer))

    block = lax.div(place_of(at()), n_u)
    total = ga[block].astype(F32)
    for n in range(1, n_dp):
        send(ga.at[0], gax.at[n], ga_sem, (n,), core_peer).wait_recv()
        total = total + gax[n].astype(F32)
    ga_out[...] = total
    total = gb[:, lanes_of(at())]
    for n in range(1, len(groups)):
        send(gbx.at[0], gbx.at[n], gb_sem, (n,), core_peer).wait_recv()
        total = total + gbx[n]
    gb_out[...] = total

    for place in range(2):
        for keep, copy in waiting[place]:

            @pl.when(jnp.logical_not(keep))
            def _():
                copy().wait_send()

    @pl.when(u == t)
    def _():
        for n, step in enumerate(steps):
            if n:
                packet(n, step).wait_send()

    for k in range(1, n_u):
        for p in range(n_pc):
            wa(k, p).wait_send()
    for kb in range(2):
        for kc_ in range(2):
            if kb or kc_:
                for j in range(n_ch):
                    scatter(kb, kc_, j).wait_send()
    for copy in sent:
        copy.wait_send()

    total = mg[block]
    for n in range(1, n_dp):
        send(mg.at[0], mgx.at[n], mg_sem, (n,), core_peer).wait_recv()
        total = total + mgx[n]
    mag_out[...] = total[0:1] / jnp.sqrt(pk[block, rank : rank + 1, :] + 1e-06)


def fused(hidden, weight_t, factor_bt, factor_a, magnitude, cotangent, n_u, n_x):
    rows, depth = hidden.shape
    cols = weight_t.shape[0]
    rank = factor_a.shape[0]
    n_blk = 4 * n_x
    n_dp = n_blk * n_u
    n_ch, n_pc = len(cuts(cols, LANES)), len(cuts(cols, PIECE))
    wide = n_x * LANES
    size_b = granule(depth, n_dp)
    groups = n_u * n_x
    few = max(n_x - 1, 1)
    sem = pltpu.SemaphoreType.DMA
    vmem = pltpu.VMEM
    whole = pl.BlockSpec(memory_space=pltpu.VMEM)
    return pl.pallas_call(
        functools.partial(kernel, n_u, n_x),
        out_shape=(
            jax.ShapeDtypeStruct(cotangent.shape, BF16),
            jax.ShapeDtypeStruct((1, cols), F32),
            jax.ShapeDtypeStruct((rank, cols), F32),
            jax.ShapeDtypeStruct((rank, size_b), F32),
        ),
        in_specs=[pl.BlockSpec(memory_space=pltpu.HBM)] * 2 + [whole] * 4,
        out_specs=(whole,) * 4,
        scratch_shapes=[
            vmem((2, 2 * rows, depth), BF16),
            vmem((n_u, n_x, cols, depth), BF16),
            vmem((2, 2 * rows, wide), F32),
            vmem((2, 2 * rows, wide), BF16),
            vmem((2 * n_ch, n_u - 1, 2 * rows, wide), BF16),
            vmem((2 * n_ch, 2, rows, wide), BF16),
            vmem((4, n_ch, rows, wide), BF16),
            vmem((8, cols), F32),
            vmem((n_u - 1, 8, cols), F32),
            vmem((rank, rows), F32),
            vmem((n_u - 1, rank, rows), F32),
            vmem((rank, rows), F32),
            vmem((n_u - 1, rank, rows), F32),
            vmem((4, rank, rows), BF16),
            vmem((n_blk, rank + 8, cols), F32),
            vmem((rank + 8, cols), F32),
            vmem((n_blk, rank, cols), BF16),
            vmem((n_dp, rank, cols), BF16),
            vmem((rank, depth), F32),
            vmem((groups, rank, size_b), F32),
            vmem((n_blk, 8, cols), F32),
            vmem((n_dp, 8, cols), F32),
            sem((2,)),
            sem((2, 1)),
            sem((2, H_CHUNK)),
            sem((2, H_CHUNK)),
            sem((2, few, n_pc)),
            sem((2, n_u - 1, n_pc)),
            sem((2, n_u - 1, few, n_pc)),
            sem((2,)),
            sem((2 * n_ch, n_u - 1)),
            sem((2, 4, n_ch)),
            sem((2, n_u - 1)),
            sem((2, n_u - 1)),
            sem((2, n_u - 1)),
            sem((2, 3)),
            sem((n_dp,)),
            sem((n_blk,)),
            sem((2, n_dp)),
            sem((2, groups)),
            sem((2, n_dp)),
        ],
        compiler_params=pltpu.CompilerParams(
            collective_id=0, has_side_effects=True, vmem_limit_bytes=67043328
        ),
        name="fused",
    )(hidden, weight_t, factor_bt, factor_a, magnitude, cotangent)


def body(hidden, weight, factor_b, factor_a, magnitude, cotangent, *, n_u, n_x):
    depth = hidden.shape[1]
    cols = weight.shape[1]
    n_dp = n_u * 4 * n_x
    mixed, mag, ga, gb = fused(
        hidden, weight.T, factor_b.T, factor_a, magnitude[None], cotangent, n_u, n_x
    )
    me = lax.axis_index(("u", "b", "x", "core"))
    share = cols // n_u
    first = lax.rem(me, n_u) * share
    share_b = depth // n_dp
    first_b = lax.rem(me * share_b, gb.shape[1])
    return (
        mixed,
        lax.dynamic_slice_in_dim(mag[0], first, share, 0),
        lax.dynamic_slice_in_dim(ga, first, share, 1),
        lax.dynamic_slice_in_dim(gb, first_b, share_b, 1).T,
    )


def solution(mesh):
    n_dp, n_u = mesh.shape["dp"], mesh.shape["tensor"]
    n_x = n_dp // (4 * n_u)
    fine = Mesh(mesh.devices.reshape(n_u, 2, n_x, 2, n_u), AXES)
    dp = ("u", "b", "x", "core")

    def step(*args):
        return body(*args, n_u=n_u, n_x=n_x)

    return jax.shard_map(
        step,
        mesh=fine,
        in_specs=(
            P(dp, "tensor"),
            P("tensor", dp),
            P("tensor", None),
            P(None, dp),
            P("tensor"),
            P(dp, "tensor"),
        ),
        out_specs=(
            P(dp, "tensor"),
            P(("tensor",) + dp),
            P(None, ("tensor",) + dp),
            P(("tensor",) + dp, None),
        ),
        check_vma=False,
    )
```

time: 535 us -> 443 us (0.83)
  Pallas kernels: 0 us -> 434 us
  blocking collectives: 264 us -> 0 us
  waiting for transfers between devices: 120 us -> 0 us
  matrix products: 54.2 us -> 0 us
  local copies, waits for them, and re-layouts: 50.8 us -> 8.1 us
  starting transfers between devices: 23.8 us -> 0 us
  between operations: 14.9 us -> 0.66 us
    pallas_call x0 -> x1, Pallas kernels: none -> 434 us  [fused(): pl.pallas_call(functools.partial(kernel, n_u, n_x), out_shape=(jax.ShapeD...]
    all_gather x1 -> x0, blocking collectives: 145 us -> none  [body(): full_a = lax.all_gather(factor_a, dp, axis=1, tiled=True)]
    unnamed x1 -> x0, blocking collectives: 80.5 us -> none
    all_to_all x2 -> x0, waiting for transfers between devices: 66.6 us -> none  [the longest x1 40.7 us: body(): got = lax.all_to_all(sends, ('tensor', 'mid', 'core'), 0, 0, tiled=True)]
    dot_general x7 -> x0, matrix products: 54.2 us -> none  [the longest x1 37.6 us: body(): sends = jnp.dot(h_rows, w_all, preferred_element_type=F32).astype(BF16)]
    all_gather x1 -> x0, waiting for transfers between devices: 52.7 us -> none  [body(): w_all = lax.all_gather(weight, 'outer', axis=1, tiled=True)]
    psum x5 -> x0, blocking collectives: 39.1 us -> none  [the longest x3 26.5 us: body(): mag_part = lax.psum(mag_part, axis)]
    all_to_all x2 -> x0, starting transfers between devices: 21.7 us -> none  [the longest x1 16.8 us: body(): parts = lax.all_to_all(parts.transpose(1, 0, 2), dp, 0, 0, tiled=True)]
  transfers between devices with their start and end apart: 6 -> 0, of which waited for: 3 -> 0; matrix products, arithmetic and copies ran while one was open for 9% -> 0% of each run, Pallas kernels for 0% -> 0%
where the time goes in v2:
time: 443 us
  Pallas kernels  434 us (98%)
  local copies, waits for them, and re-layouts  8.1 us (2%)
    pallas_call x1, Pallas kernels, fused(): pl.pallas_call(functools.partial(kernel, n_u, n_x), out_shape=(jax.ShapeD...  434 us

profile of v2, /device:TPU:4, one launch (start us, length us, event | category | flops | bytes accessed | tf_op | source)
XLA Modules:
  0.0 442.9 jit_solution(9096914737530554368)
XLA Ops:
  0.6 1.3 broadcast_in_dim.3.mag
  2.0 434.2 %fused.1 = (bf16[320,2304]{1,0:T(8,128)(2,1)}, f32[1,288]{1,0:T(1,128)}, f32[16,288]{1,0:T(8,128)}, f32[16,1152]{1,0:T(8,128)}) custom-call(bf16[320,9216]{1,0:T(8,128)(2,1)} %h.1, bf16[288,9216]{1,0:T(8,128)(2,1)} %bitcast.5, bf16[16,9216]{1,0:T(8,128)(2,1)} %bitcast.6, bf16[16,288]{1,0:T(8,128)(2,1)} %a.1, f32[1,2304]{1,0:T(1,128)} %broadcast_in_dim.3.mag, ...), custom_call_target="tpu_custom_call" | custom-call | tf_op jit(solution)/shard_map/fused/pallas_call | solution.py:507
  436.1 1.4 constant_dynamic-slice_fusion
  437.6 1.3 constant_dynamic-slice_fusion.1
  438.9 1.5 dynamic-slice_bitcast_fusion
  440.4 2.6 copy.11

commit v3 on v2

v3 whole, which is shorter than its diff:
```python
import functools

import jax
import jax.numpy as jnp
from jax import lax
from jax.experimental import pallas as pl
from jax.experimental.pallas import tpu as pltpu
from jax.sharding import Mesh, PartitionSpec as P

F32, BF16 = jnp.float32, jnp.bfloat16
AXES = ("u", "b", "x", "core", "tensor")
MESH = pl.DeviceIdType.MESH
NT = (((1,), (1,)), ((), ()))
NN = (((1,), (0,)), ((), ()))
TN = (((0,), (0,)), ((), ()))
H_CHUNK = 6
LATE_CHUNK = 2
LATE_SHARE = 10
PIECE = 32
LANES = 128


def split_of(size, most):
    best = LANES
    for step in range(LANES, most + 1, LANES):
        if size % step == 0:
            best = step
    return best


def cuts(size, step):
    return [(at, min(step, size - at)) for at in range(0, size, step)]


def chunks_of(cols, n_x):
    rest = cuts(cols - LANES, LANES // n_x)
    return [(0, LANES)] + [(LANES + at, size) for at, size in rest]


def pieces_of(cols, n_x):
    last = chunks_of(cols, n_x)[-1][0]
    return cuts(last, PIECE) + [(last + at, size) for at, size in cuts(cols - last, PIECE // 2)]


def granule(depth, n_dp):
    share = depth // n_dp
    size = share
    while size % LANES:
        size += share
    return size


def padded(lanes):
    return -(-lanes // LANES) * LANES


def dot(left, right, dims):
    return lax.dot_general(left, right, dims, preferred_element_type=F32)


def kernel(
    n_u, n_x, h, w, bt, a, mag, cot, mixed, mag_out, ga_out, gb_out,
    hs, ws, own, part_out, part_in, scat, late_sum, late_own, late_out, late_in, got_out, sq, sqx, low, lowx, back, backx, backs, pk_a, pk_s, pks,
    ga, gax, gb, gbx, mg, mgx,
    loc_sem, hc_sem, hb_sem, hr_sem, wx_sem, wa_sem, wr_sem, ps_sem, pr_sem, sc_sem, ls_sem, lr_sem, lsc_sem, turn_sem,
    sq_sem, low_sem, back_sem, tok_sem, pk_ssem, pk_rsem, ga_sem, gb_sem, mg_sem,
):
    u, b, x, c, t = (lax.axis_index(name) for name in AXES)
    rows, depth = h.shape
    cols = w.shape[0]
    rank = a.shape[0]
    n_blk = 4 * n_x
    n_dp = n_blk * n_u
    late = rows // LATE_SHARE
    soon = rows - late
    kc = split_of(depth, 1152)
    n_h = H_CHUNK + LATE_CHUNK
    h_cuts = [(i * (soon // H_CHUNK), soon // H_CHUNK) for i in range(H_CHUNK)]
    h_cuts += [(soon + i * (late // LATE_CHUNK), late // LATE_CHUNK) for i in range(LATE_CHUNK)]
    chunks = chunks_of(cols, n_x)
    pieces = pieces_of(cols, n_x)
    n_ch, n_pc = len(chunks), len(pieces)

    def at(**moved):
        here = dict(u=u, b=b, x=x, core=c, tensor=t)
        here.update(moved)
        return tuple(here[name] for name in AXES)

    def shift(value, by, n):
        return lax.rem(value + by, n)

    def remote(src, dst, send_sem, recv_sem, peer):
        return pltpu.make_async_remote_copy(
            src_ref=src, dst_ref=dst, send_sem=send_sem, recv_sem=recv_sem, device_id=peer, device_id_type=MESH
        )

    def send(src, dst, sems, index, peer):
        return remote(src, dst, sems.at[(0,) + index], sems.at[(1,) + index], peer)

    core_peer = at(core=1 - c)
    b_peer = at(b=1 - b)
    x_to = [at(x=shift(x, k, n_x)) for k in range(n_x)]
    u_to = [at(u=shift(u, k, n_u), b=shift(b, k % 2, 2)) for k in range(n_u)]
    t_to = [at(tensor=shift(t, k, n_u)) for k in range(n_u)]
    steps = [(i, j, k, l) for i in range(n_u) for j in range(2) for k in range(n_x) for l in range(2)]

    def moved(step):
        du, db, dx, dc = step
        return at(u=shift(u, du, n_u), b=shift(b, db, 2), x=shift(x, dx, n_x), core=shift(c, dc, 2))

    def place_of(device):
        return ((device[0] * 2 + device[1]) * n_x + device[2]) * 2 + device[3]

    def block_of(bb, xx, cc):
        return (bb * n_x + xx) * 2 + cc

    far = shift(b, u - t + n_u, 2)

    peers = [moved(step) for step in steps[1:]] + t_to[1:]
    barrier = pltpu.get_barrier_semaphore()
    for peer in peers:
        pl.semaphore_signal(barrier, inc=1, device_id=peer, device_id_type=MESH)
    pl.semaphore_wait(barrier, len(peers))

    def row_of(kb, cc, first):
        return kb * 2 * rows + (cc * soon + first if first < soon else 2 * soon + cc * late + first - soon)

    def rows_at(kb, cc, first, size):
        return pl.ds(pl.multiple_of(row_of(kb, cc, first), 16), size)

    halves = [(0, soon), (soon, late)]

    def h_rows(kb, cc, i):
        return hs.at[rows_at(kb, cc, *h_cuts[i]), :]

    def w_rows(uu, xx, p):
        first, size = pieces[p]
        return ws.at[uu, xx, pl.ds(first, size), :]

    def half_rows(cc, half):
        return hs.at[rows_at(0, cc, *halves[half]), :]

    sent = []

    def start(copy):
        copy.start()
        sent.append(copy)

    def late_h(i):
        return send(h.at[pl.ds(*h_cuts[i]), :], h_rows(1, c, i), hb_sem, (i,), b_peer)

    def start_h(i):
        start(late_h(i))

    def start_wx(p):
        first, size = pieces[p]
        for k in range(1, n_x):
            start(send(w.at[pl.ds(first, size), :], w_rows(u, x, p), wx_sem, (k - 1, p), x_to[k]))

    def wa(k, p):
        first, size = pieces[p]
        return send(w.at[pl.ds(first, size), :], w_rows(u, x, p), wa_sem, (k - 1, p), u_to[k])

    def start_wa(p):
        for k in range(1, n_u):
            wa(k, p).start()

    early = lax.rem(u, 2) != b

    loads = [
        pltpu.make_async_copy(w, ws.at[u, x], loc_sem.at[1]),
    ] + [
        pltpu.make_async_copy(h.at[pl.ds(*halves[i]), :], half_rows(c, i), loc_sem.at[2 * i]) for i in range(2)
    ]
    for load in loads:
        load.start()
    for i in range(2):
        start(send(h.at[pl.ds(*halves[i]), :], half_rows(c, i), hc_sem, (i,), core_peer))
    start_h(0)
    for p in range(2):
        start_wx(p)

    @pl.when(early)
    def _():
        for p in range(2):
            start_wa(p)

    loads[0].wait()
    a_t = jnp.transpose(a[...].astype(F32)).astype(BF16)

    def square_step(i, acc):
        at_k = pl.ds(pl.multiple_of(i * kc, LANES), kc)
        merged = ws[u, x, :, at_k].astype(F32) + dot(a_t, bt[:, at_k], NN)
        for g in range(kc // LANES):
            part = merged[:, g * LANES : (g + 1) * LANES]
            acc = acc + part * part
        return acc

    squares = lax.fori_loop(0, depth // kc, square_step, jnp.zeros((cols, LANES), F32))
    sq[...] = lax.dot_general(
        jnp.ones((8, LANES), F32), squares, NT, precision=lax.Precision.HIGHEST, preferred_element_type=F32
    )
    for k in range(1, n_u):
        start(send(sq, sqx.at[k - 1], sq_sem, (k - 1,), t_to[k]))

    loads[1].wait()
    loads[2].wait()

    def low_step(i, acc):
        at_k = pl.ds(pl.multiple_of(i * kc, LANES), kc)
        left = jnp.concatenate([hs[rows_at(0, c, *half), at_k] for half in halves], axis=0)
        return acc + dot(bt[:, at_k], left, NT)

    low[...] = lax.fori_loop(0, depth // kc, low_step, jnp.zeros((rank, rows), F32))
    for k in range(1, n_u):
        start(send(low, lowx.at[k - 1], low_sem, (k - 1,), t_to[k]))

    def from_t(ref, extra, sems):
        total = ref[...]
        for k in range(1, n_u):
            send(ref, extra.at[k - 1], sems, (k - 1,), t_to[k]).wait_recv()
            total = total + extra[k - 1]
        return total

    square_sum = from_t(sq, sqx, sq_sem)
    mine = block_of(b, x, c)

    def packet(n, step):
        return [
            remote(a, pk_a.at[mine], pk_ssem.at[0, n], pk_rsem.at[0, n % n_blk], moved(step)),
            remote(pks, pk_s.at[mine], pk_ssem.at[1, n], pk_rsem.at[1, n % n_blk], moved(step)),
        ]

    @pl.when(u == t)
    def _():
        pks[...] = square_sum[0:1, :]
        pk_a[mine] = a[...]
        pk_s[mine] = square_sum[0:1, :]
        for n, step in enumerate(steps):
            if n:
                for copy in packet(n, step):
                    copy.start()

    for i in range(1, 3):
        start_h(i)
    for p in range(2, 4):
        start_wx(p)

    @pl.when(early)
    def _():
        for p in range(2, 4):
            start_wa(p)

    low_t = from_t(low, lowx, low_sem)
    low_tb = low_t.astype(BF16)
    low_b = jnp.transpose(low_t).astype(BF16)

    count = [0]
    waiting = [[], []]

    def lag_of(uu):
        return lax.rem(uu - t + 2 * n_u - 1, n_u)

    def lanes_in(j):
        first, size = chunks[j]
        return pl.ds(n_x * first, padded(n_x * size))

    spans = {0: (0, 2 * rows), 1: (2 * rows, 2 * soon), 2: (0, 2 * (rows + soon))}

    def run_unit(kb, ku, j):
        first, size = chunks[j]
        wide = n_x * size
        top, tall = spans[kb]
        place = count[0] % 2
        count[0] += 1
        uu = shift(u, ku, n_u)
        keep = uu == t

        def copy():
            return remote(
                part_out.at[place, 0:tall, 0 : padded(wide)], part_in.at[lag_of(uu), top : top + tall, lanes_in(j)],
                ps_sem.at[place], pr_sem.at[min(kb, 1), j, lag_of(uu)], at(tensor=uu),
            )

        if waiting[place]:
            old_keep, old_copy = waiting[place].pop()

            @pl.when(jnp.logical_not(old_keep))
            def _():
                old_copy().wait_send()

        own[place, 0:tall, 0:wide] = jnp.zeros((tall, wide), F32)

        def unit_step(i, carry):
            at_k = pl.ds(pl.multiple_of(i * kc, LANES), kc)
            right = jnp.concatenate([ws[uu, xx, first : first + size, at_k] for xx in range(n_x)], axis=0)
            own[place, 0:tall, 0:wide] += dot(hs[top : top + tall, at_k], right, NT)
            return carry

        lax.fori_loop(0, depth // kc, unit_step, 0)

        @pl.when(jnp.logical_not(keep))
        def _():
            part_out[place, 0:tall, 0:wide] = own[place, 0:tall, 0:wide].astype(BF16)
            copy().start()

        waiting[place].append((keep, copy))
        return kb, uu, j, place

    def scatter(kb, kc_, j):
        index = (kb * 2 + kc_, j)
        span = pl.ds(0, soon if kb else rows)
        return send(
            scat.at[kb * 2 + kc_, span, lanes_in(j)], got_out.at[far * 2 + c, span, lanes_in(j)], sc_sem, index,
            at(b=shift(b, kb, 2), core=shift(c, kc_, 2)),
        )

    def finish(kb, uu, j, place):
        first, size = chunks[j]
        wide = n_x * size
        top, tall = spans[kb]
        lanes = pl.ds(n_x * first, wide)

        @pl.when(uu == t)
        def _():
            for k in range(n_u - 1):
                remote(
                    part_out.at[0, 0:tall, 0 : padded(wide)], part_in.at[k, top : top + tall, lanes_in(j)],
                    ps_sem.at[0], pr_sem.at[min(kb, 1), j, k], t_to[1],
                ).wait_recv()
            for side in (0, 1) if kb == 2 else (kb,):
                for kc_ in range(2):
                    for half in halves[: 1 if side else 2]:
                        at_c = row_of(side, shift(c, kc_, 2), half[0])
                        total = own[place, pl.ds(pl.multiple_of(at_c - top, 16), half[1]), 0:wide]
                        for k in range(n_u - 1):
                            more = part_in[k, pl.ds(pl.multiple_of(at_c, 16), half[1]), lanes]
                            total = total + more.astype(F32)
                        if side == 0 and kc_ == 0:
                            got_out[far * 2 + c, pl.ds(*half), lanes] = total.astype(BF16)
                        else:
                            scat[side * 2 + kc_, pl.ds(*half), lanes] = total.astype(BF16)
                    if side or kc_:
                        scatter(side, kc_, j).start()

    pending = []

    def go(kb, ku, j):
        new = run_unit(kb, ku, j)
        if pending:
            finish(*pending.pop())
        pending.append(new)

    def late_part(uu):
        return remote(late_out, late_in.at[lag_of(uu)], ls_sem.at[0], lr_sem.at[lag_of(uu)], at(tensor=uu))

    def late_unit(uu):
        late_sum[...] = jnp.zeros(late_sum.shape, F32)

        def late_step(i, carry):
            at_k = pl.ds(pl.multiple_of(i * kc, LANES), kc)
            right = jnp.concatenate(
                [ws[uu, xx, first : first + size, at_k] for first, size in chunks for xx in range(n_x)], axis=0
            )
            late_sum[...] += dot(right, hs[2 * (rows + soon) : 4 * rows, at_k], NT)
            return carry

        lax.fori_loop(0, depth // kc, late_step, 0)
        return jnp.transpose(late_sum[...])

    def late_scatter(kc_):
        return send(
            scat.at[2 + kc_, pl.ds(soon, late), :], got_out.at[far * 2 + c, pl.ds(soon, late), :], lsc_sem, (kc_,),
            at(b=1 - b, core=shift(c, kc_, 2)),
        )

    passed = [0]

    def pass_h():
        i = passed[0]
        passed[0] += 1
        got = h_rows(1, c, i)
        send(got, got, hb_sem, (i,), b_peer).wait_recv()
        start(send(got, got, hr_sem, (i,), core_peer))

    def near(p):
        for k in range(1, n_x):
            got = w_rows(u, shift(x, n_x - k, n_x), p)
            send(got, got, wx_sem, (k - 1, p), x_to[k]).wait_recv()

    def of_chunk(j):
        first, size = chunks[j]
        return [p for p in range(n_pc) if first <= pieces[p][0] < first + size]

    for q in range(n_blk):
        _, db, dx, dc = steps[q]
        src = block_of(shift(b, db, 2), shift(x, n_x - dx, n_x), shift(c, dc, 2))
        for wait in (
            remote(a, pk_a.at[src], pk_ssem.at[0, 0], pk_rsem.at[0, q], core_peer),
            remote(pks, pk_s.at[src], pk_ssem.at[1, 0], pk_rsem.at[1, q], core_peer),
        ):
            if q:
                wait.wait_recv()
            else:
                pl.when(u != t)(wait.wait_recv)

    def scale_of(i, first, size):
        norm = jnp.sqrt(pk_s[i, 0:1, first : first + size] + 1e-06)
        return mag[:, i * cols + first : i * cols + first + size] / norm

    back_part = jnp.zeros((rank, rows), F32)
    for i in range(n_blk):
        piece = cot[:, i * cols : (i + 1) * cols].astype(F32)
        dpre = (piece * scale_of(i, 0, cols)).astype(BF16)
        back_part = back_part + dot(pk_a[i], dpre, NT)
        ga[i] = dot(low_tb, dpre, NN).astype(BF16)
    back[...] = back_part
    for k in range(1, n_u):
        start(send(back, backx.at[k - 1], back_sem, (k - 1,), t_to[k]))
    for n, step in enumerate(steps):
        if n:
            peer = moved(step)
            start(send(ga.at[lax.div(place_of(peer), n_u)], gax.at[n], ga_sem, (n,), peer))
    back_b = from_t(back, backx, back_sem).astype(BF16)
    backs[c] = back_b
    for k in range(1, 4):
        peer = at(b=shift(b, k // 2, 2), core=shift(c, k % 2, 2))
        start(send(backs.at[c], backs.at[k // 2 * 2 + c], tok_sem, (k - 1,), peer))

    for i in range(3, H_CHUNK):
        start_h(i)
    for p in range(4, n_pc):
        start_wx(p)

    @pl.when(early)
    def _():
        for p in range(4, n_pc):
            start_wa(p)

    for i in range(2):
        send(half_rows(1 - c, i), half_rows(1 - c, i), hc_sem, (i,), core_peer).wait_recv()

    def turn(peer):
        pl.semaphore_signal(turn_sem, inc=1, device_id=peer, device_id_type=MESH)

    def w_arrived(k, p):
        got = w_rows(shift(u, n_u - k, n_u), x, p)
        send(got, got, wa_sem, (k - 1, p), u_to[k]).wait_recv()
        for m in range(1, n_x):
            send(got, got, wr_sem, (k - 1, m - 1, p), x_to[m]).start()

    for j in range(n_ch):
        while passed[0] < H_CHUNK * (j + 1) // n_ch:
            pass_h()
        for p in of_chunk(j):
            near(p)
        if j >= n_ch - 2:

            @pl.when(early)
            def _():
                for k in range(1, n_u):
                    for p in range(n_pc):
                        if (p in of_chunk(n_ch - 1)) == (j == n_ch - 1):
                            w_arrived(k, p)
                if j == n_ch - 1:
                    turn(at(u=shift(u, 1, n_u)))

        if j == n_ch - 1:

            @pl.when(jnp.logical_not(early))
            def _():
                pl.semaphore_wait(turn_sem, 1)
                for p in range(n_pc):
                    start_wa(p)
                for i in range(H_CHUNK, n_h):
                    late_h(i).start()

        go(0, 0, j)
    for i in range(H_CHUNK):
        got = h_rows(1, 1 - c, i)
        send(got, got, hr_sem, (i,), core_peer).wait_recv()

    for k in range(1, 4):
        src = k // 2 * 2 + shift(c, k % 2, 2)
        send(backs.at[src], backs.at[src], tok_sem, (k - 1,), core_peer).wait_recv()

    def grad_of(kb, half, at_k):
        first, size = halves[half]
        total = jnp.zeros((rank, kc), F32)
        for cc in range(2):
            held = hs[row_of(kb, cc, first) : row_of(kb, cc, first) + size, at_k]
            total = total + dot(backs[kb * 2 + cc, :, first : first + size], held, NN)
        return total

    def grad_step(i, carry):
        at_k = pl.ds(pl.multiple_of(i * kc, LANES), kc)
        total = jnp.zeros((rank, kc), F32)
        for kb, half in ((0, 0), (0, 1), (1, 0)):
            total = total + grad_of(kb, half, at_k)
        gb[:, at_k] = total
        return carry

    lax.fori_loop(0, depth // kc, grad_step, 0)
    size_b = granule(depth, n_dp)
    share_b = depth // n_dp

    def lanes_of(device):
        return pl.ds(pl.multiple_of(lax.div(place_of(device) * share_b, size_b) * size_b, LANES), size_b)

    groups = [step for step in steps if step[1] == 0 and step[3] == 0]
    def far_piece(k, p):
        @pl.when(jnp.logical_not(early))
        def _():
            w_arrived(k, p)
            if k == n_u - 1 and p == n_pc - 1:
                turn(b_peer)

    def far_ready(k, j):
        for p in of_chunk(j):
            for m in range(1, n_x):
                got = w_rows(shift(u, n_u - k, n_u), shift(x, n_x - m, n_x), p)
                send(got, got, wr_sem, (k - 1, m - 1, p), x_to[m]).wait_recv()

    units = [(1, 0, j) for j in range(n_ch)]
    for k in range(1, n_u):
        for p in range(n_pc):
            done = [j for j in range(n_ch) if max(of_chunk(j)) == p - 1]
            if units and not (k == n_u - 1 and p == n_pc - 1):
                go(*units.pop(0))
            far_piece(k, p)
            for j in done:
                far_ready(k, j)
                units.append((2, n_u - k, j))
        if k == n_u - 1:
            while units:
                go(*units.pop(0))

            @pl.when(early)
            def _():
                pl.semaphore_wait(turn_sem, 1)
                for i in range(H_CHUNK, n_h):
                    late_h(i).start()

        far_ready(k, n_ch - 1)
        units.append((2, n_u - k, n_ch - 1))
    for unit in units:
        go(*unit)
    finish(*pending.pop())

    for i in range(H_CHUNK, n_h):
        pass_h()
    for i in range(H_CHUNK, n_h):
        got = h_rows(1, 1 - c, i)
        send(got, got, hr_sem, (i,), core_peer).wait_recv()
    for k in range(1, n_u):
        if k > 1:
            late_part(shift(t, k - 1, n_u)).wait_send()
        late_out[:, 0 : n_x * cols] = late_unit(shift(t, k, n_u)).astype(BF16)
        late_part(shift(t, k, n_u)).start()

    def grad_late(i, carry):
        at_k = pl.ds(pl.multiple_of(i * kc, LANES), kc)
        gb[:, at_k] += grad_of(1, 1, at_k)
        return carry

    lax.fori_loop(0, depth // kc, grad_late, 0)
    for n, step in enumerate(groups):
        if n:
            peer = moved(step)
            start(send(gb.at[:, lanes_of(peer)], gbx.at[n], gb_sem, (n,), peer))
    late_own[:, 0 : n_x * cols] = late_unit(t)

    def emit(bb, cc, j, half):
        first, size = chunks[j]
        span = pl.ds(*halves[half])
        for xx in range(n_x):
            i = block_of(bb, xx, cc)
            left = i * cols + first
            lane = n_x * first + xx * size
            pre = got_out[bb * 2 + cc, span, lane : lane + size].astype(F32)
            low_half = low_b[halves[half][0] : sum(halves[half]), :]
            pre = pre + dot(low_half, pk_a[i, :, first : first + size], NN)
            mixed[span, left : left + size] = (pre * scale_of(i, first, size)).astype(BF16)
            part = jnp.sum(cot[span, left : left + size].astype(F32) * pre, axis=0, keepdims=True)
            if half:
                mg[i, 0:1, first : first + size] += part
            else:
                mg[i, 0:1, first : first + size] = part

    def soon_outputs(bb):
        for cc in range(2):
            for j in range(n_ch):
                kind = lax.rem(bb + far, 2) * 2 + lax.rem(cc + c, 2)

                def scattered(span):
                    got = got_out.at[bb * 2 + cc, span, lanes_in(j)]
                    return send(got, got, sc_sem, (kind, j), core_peer)

                @pl.when(jnp.logical_and(bb == far, cc != c))
                def _():
                    scattered(pl.ds(0, rows)).wait_recv()

                @pl.when(bb != far)
                def _():
                    scattered(pl.ds(0, soon)).wait_recv()

                emit(bb, cc, j, 0)

                @pl.when(bb == far)
                def _():
                    emit(bb, cc, j, 1)

    soon_outputs(0)
    for k in range(n_u - 1):
        remote(late_out, late_in.at[k], ls_sem.at[0], lr_sem.at[k], t_to[1]).wait_recv()
    for kc_ in range(2):
        at_c = pl.ds(pl.multiple_of(shift(c, kc_, 2) * late, 16), late)
        total = late_own[at_c, 0 : n_x * cols]
        for k in range(n_u - 1):
            total = total + late_in[k, at_c, 0 : n_x * cols].astype(F32)
        scat[2 + kc_, pl.ds(soon, late), 0 : n_x * cols] = total.astype(BF16)
        late_scatter(kc_).start()
    soon_outputs(1)
    for kc_ in range(2):
        got = got_out.at[(1 - far) * 2 + shift(c, kc_, 2), pl.ds(soon, late), :]
        send(got, got, lsc_sem, (kc_,), core_peer).wait_recv()
    for bb in range(2):

        @pl.when(bb != far)
        def _():
            for cc in range(2):
                for j in range(n_ch):
                    emit(bb, cc, j, 1)

    for n, step in enumerate(steps):
        if n:
            peer = moved(step)
            start(send(mg.at[lax.div(place_of(peer), n_u)], mgx.at[n], mg_sem, (n,), peer))

    block = lax.div(place_of(at()), n_u)
    total = ga[block].astype(F32)
    for n in range(1, n_dp):
        send(ga.at[0], gax.at[n], ga_sem, (n,), core_peer).wait_recv()
        total = total + gax[n].astype(F32)
    share = cols // n_u
    for q in range(n_u):

        @pl.when(lax.rem(place_of(at()), n_u) == q)
        def _():
            ga_out[...] = total[:, q * share : (q + 1) * share]

    total = gb[:, lanes_of(at())]
    for n in range(1, len(groups)):
        send(gbx.at[0], gbx.at[n], gb_sem, (n,), core_peer).wait_recv()
        total = total + gbx[n]
    for q in range(size_b // share_b):

        @pl.when(lax.rem(place_of(at()), size_b // share_b) == q)
        def _():
            gb_out[...] = total[:, q * share_b : (q + 1) * share_b]

    for place in range(2):
        for keep, copy in waiting[place]:

            @pl.when(jnp.logical_not(keep))
            def _():
                copy().wait_send()

    @pl.when(u == t)
    def _():
        for n, step in enumerate(steps):
            if n:
                for copy in packet(n, step):
                    copy.wait_send()

    for k in range(1, n_u):
        for p in range(n_pc):
            wa(k, p).wait_send()
            got = w_rows(shift(u, n_u - k, n_u), x, p)
            for m in range(1, n_x):
                send(got, got, wr_sem, (k - 1, m - 1, p), x_to[m]).wait_send()
    for i in range(H_CHUNK, n_h):
        late_h(i).wait_send()
    late_part(shift(t, n_u - 1, n_u)).wait_send()
    for kc_ in range(2):
        late_scatter(kc_).wait_send()
    for kb in range(2):
        for kc_ in range(2):
            if kb or kc_:
                for j in range(n_ch):
                    scatter(kb, kc_, j).wait_send()
    for copy in sent:
        copy.wait_send()

    total = mg[block]
    for n in range(1, n_dp):
        send(mg.at[0], mgx.at[n], mg_sem, (n,), core_peer).wait_recv()
        total = total + mgx[n]
    total = total / jnp.sqrt(pk_s[block] + 1e-06)
    for q in range(n_u):

        @pl.when(lax.rem(place_of(at()), n_u) == q)
        def _():
            mag_out[...] = total[:, q * share : (q + 1) * share]


def fused(hidden, weight_t, factor_bt, factor_a, magnitude, cotangent, n_u, n_x):
    rows, depth = hidden.shape
    cols = weight_t.shape[0]
    rank = factor_a.shape[0]
    n_blk = 4 * n_x
    n_dp = n_blk * n_u
    n_ch, n_pc = len(chunks_of(cols, n_x)), len(pieces_of(cols, n_x))
    wide = n_x * LANES
    full = padded(n_x * cols)
    late = rows // LATE_SHARE
    n_h = H_CHUNK + LATE_CHUNK
    size_b = granule(depth, n_dp)
    groups = n_u * n_x
    few = max(n_x - 1, 1)
    sem = pltpu.SemaphoreType.DMA
    vmem = pltpu.VMEM
    whole = pl.BlockSpec(memory_space=pltpu.VMEM)
    return pl.pallas_call(
        functools.partial(kernel, n_u, n_x),
        out_shape=(
            jax.ShapeDtypeStruct(cotangent.shape, BF16),
            jax.ShapeDtypeStruct((1, cols // n_u), F32),
            jax.ShapeDtypeStruct((rank, cols // n_u), F32),
            jax.ShapeDtypeStruct((rank, depth // n_dp), F32),
        ),
        in_specs=[pl.BlockSpec(memory_space=pltpu.HBM)] * 2 + [whole] * 4,
        out_specs=(whole,) * 4,
        scratch_shapes=[
            vmem((4 * rows, depth), BF16),
            vmem((n_u, n_x, cols, depth), BF16),
            vmem((2, 4 * rows - 2 * late, wide), F32),
            vmem((2, 4 * rows - 2 * late, wide), BF16),
            vmem((n_u - 1, 4 * rows - 2 * late, full), BF16),
            vmem((4, rows, full), BF16),
            vmem((n_x * cols, 2 * late), F32),
            vmem((2 * late, full), F32),
            vmem((2 * late, full), BF16),
            vmem((n_u - 1, 2 * late, full), BF16),
            vmem((4, rows, full), BF16),
            vmem((8, cols), F32),
            vmem((n_u - 1, 8, cols), F32),
            vmem((rank, rows), F32),
            vmem((n_u - 1, rank, rows), F32),
            vmem((rank, rows), F32),
            vmem((n_u - 1, rank, rows), F32),
            vmem((4, rank, rows), BF16),
            vmem((n_blk, rank, cols), BF16),
            vmem((n_blk, 1, cols), F32),
            vmem((1, cols), F32),
            vmem((n_blk, rank, cols), BF16),
            vmem((n_dp, rank, cols), BF16),
            vmem((rank, depth), F32),
            vmem((groups, rank, size_b), F32),
            vmem((n_blk, 1, cols), F32),
            vmem((n_dp, 1, cols), F32),
            sem((3,)),
            sem((2, 2)),
            sem((2, n_h)),
            sem((2, n_h)),
            sem((2, few, n_pc)),
            sem((2, n_u - 1, n_pc)),
            sem((2, n_u - 1, few, n_pc)),
            sem((2,)),
            sem((2, n_ch, n_u - 1)),
            sem((2, 4, n_ch)),
            sem((1,)),
            sem((n_u - 1,)),
            sem((2, 2)),
            pltpu.SemaphoreType.REGULAR,
            sem((2, n_u - 1)),
            sem((2, n_u - 1)),
            sem((2, n_u - 1)),
            sem((2, 3)),
            sem((2, n_dp)),
            sem((2, n_blk)),
            sem((2, n_dp)),
            sem((2, groups)),
            sem((2, n_dp)),
        ],
        compiler_params=pltpu.CompilerParams(
            collective_id=0, has_side_effects=True, vmem_limit_bytes=67043328
        ),
        name="fused",
    )(hidden, weight_t, factor_bt, factor_a, magnitude, cotangent)


def body(hidden, weight, factor_b, factor_a, magnitude, cotangent, *, n_u, n_x):
    mixed, mag, ga, gb = fused(
        hidden, weight.T, factor_b.T, factor_a, magnitude[None], cotangent, n_u, n_x
    )
    return mixed, mag[0], ga, gb.T


def solution(mesh):
    n_dp, n_u = mesh.shape["dp"], mesh.shape["tensor"]
    n_x = n_dp // (4 * n_u)
    fine = Mesh(mesh.devices.reshape(n_u, 2, n_x, 2, n_u), AXES)
    dp = ("u", "b", "x", "core")

    def step(*args):
        return body(*args, n_u=n_u, n_x=n_x)

    return jax.shard_map(
        step,
        mesh=fine,
        in_specs=(
            P(dp, "tensor"),
            P("tensor", dp),
            P("tensor", None),
            P(None, dp),
            P("tensor"),
            P(dp, "tensor"),
        ),
        out_specs=(
            P(dp, "tensor"),
            P(("tensor",) + dp),
            P(None, ("tensor",) + dp),
            P(("tensor",) + dp, None),
        ),
        check_vma=False,
    )
```

time: 443 us -> 314 us (0.71)
  Pallas kernels: 434 us -> 305 us
    pallas_call x1, Pallas kernels: 434 us -> 305 us  [fused(): pl.pallas_call(functools.partial(kernel, n_u, n_x), out_shape=(jax.ShapeD...]
where the time goes in v3:
time: 314 us; the launch traced here: 312 us
  Pallas kernels  305 us (97%)
  local copies, waits for them, and re-layouts  5.7 us (2%)
    pallas_call x1, Pallas kernels, fused(): pl.pallas_call(functools.partial(kernel, n_u, n_x), out_shape=(jax.ShapeD...  305 us

profile of v3, /device:TPU:4, one launch (start us, length us, event | category | flops | bytes accessed | tf_op | source)
XLA Modules:
  0.0 311.9 jit_solution(15540144079422201746)
XLA Ops:
  0.6 1.3 broadcast_in_dim.3.mag
  1.9 305.5 %fused.1 = (bf16[320,2304]{1,0:T(8,128)(2,1)}, f32[1,144]{1,0:T(1,128)}, f32[16,144]{1,0:T(8,128)}, f32[16,576]{1,0:T(8,128)}) custom-call(bf16[320,9216]{1,0:T(8,128)(2,1)} %h.1, bf16[288,9216]{1,0:T(8,128)(2,1)} %bitcast.4, bf16[16,9216]{1,0:T(8,128)(2,1)} %bitcast.5, bf16[16,288]{1,0:T(8,128)(2,1)} %a.1, f32[1,2304]{1,0:T(1,128)} %broadcast_in_dim.3.mag, ...), custom_call_target="tpu_custom_call" | custom-call | tf_op jit(solution)/shard_map/fused/pallas_call | solution.py:724
  307.4 0.0 copy-start.2
  307.4 0.0 copy-start.1
  307.5 0.0 copy-start
  307.5 2.6 copy.14
  310.1 0.0 copy-done.2
  310.1 0.6 copy.15
  310.6 0.0 copy-done.1
  310.6 0.6 copy.16
  311.2 0.0 copy-done
  311.2 0.6 copy.17
Async XLA Ops:
  307.4 2.6 copy-start.2
  307.4 3.2 %copy-start.1 = (f32[16,144]{1,0:T(8,128)S(1)}, f32[16,144]{1,0:T(8,128)}, u32[]{:S(2)}) copy-start(f32[16,144]{1,0:T(8,128)} %get-tuple-element.18) | copy-start | bytes 27652
  307.5 3.8 %copy-start = (f32[16,576]{1,0:T(8,128)S(1)}, f32[16,576]{1,0:T(8,128)}, u32[]{:S(2)}) copy-start(f32[16,576]{1,0:T(8,128)} %get-tuple-element.11) | copy-start | bytes 110596

commit v4 on v3

--- a/solution.py
+++ b/solution.py
@@ -13,10 +13,9 @@
 NT = (((1,), (1,)), ((), ()))
 NN = (((1,), (0,)), ((), ()))
 TN = (((0,), (0,)), ((), ()))
-H_CHUNK = 6
-LATE_CHUNK = 2
-LATE_SHARE = 10
-PIECE = 32
+H_PIECE = 48
+LATE_SHARE = 20
+PIECE = 16
 LANES = 128
 
 
@@ -33,13 +32,11 @@
 
 
 def chunks_of(cols, n_x):
-    rest = cuts(cols - LANES, LANES // n_x)
-    return [(0, LANES)] + [(LANES + at, size) for at, size in rest]
-
-
-def pieces_of(cols, n_x):
-    last = chunks_of(cols, n_x)[-1][0]
-    return cuts(last, PIECE) + [(last + at, size) for at, size in cuts(cols - last, PIECE // 2)]
+    last = LANES // n_x
+    rest = cols - LANES
+    if rest <= last:
+        return [(0, LANES), (LANES, rest)]
+    return [(0, LANES), (LANES, rest - last), (cols - last, last)]
 
 
 def granule(depth, n_dp):
@@ -74,12 +71,13 @@
     late = rows // LATE_SHARE
     soon = rows - late
     kc = split_of(depth, 1152)
-    n_h = H_CHUNK + LATE_CHUNK
-    h_cuts = [(i * (soon // H_CHUNK), soon // H_CHUNK) for i in range(H_CHUNK)]
-    h_cuts += [(soon + i * (late // LATE_CHUNK), late // LATE_CHUNK) for i in range(LATE_CHUNK)]
+    h_cuts = cuts(soon, H_PIECE) + [(soon, late)]
+    n_h = len(h_cuts)
+    n_soon = n_h - 1
     chunks = chunks_of(cols, n_x)
-    pieces = pieces_of(cols, n_x)
+    pieces = cuts(cols, PIECE)
     n_ch, n_pc = len(chunks), len(pieces)
+    lane_at = [sum(padded(n_x * size) for _, size in chunks[:j]) for j in range(n_ch)]
 
     def at(**moved):
         here = dict(u=u, b=b, x=x, core=c, tensor=t)
@@ -177,12 +175,12 @@
     for i in range(2):
         start(send(h.at[pl.ds(*halves[i]), :], half_rows(c, i), hc_sem, (i,), core_peer))
     start_h(0)
-    for p in range(2):
+    for p in range(4):
         start_wx(p)
 
     @pl.when(early)
     def _():
-        for p in range(2):
+        for p in range(4):
             start_wa(p)
 
     loads[0].wait()
@@ -243,12 +241,12 @@
 
     for i in range(1, 3):
         start_h(i)
-    for p in range(2, 4):
+    for p in range(4, 8):
         start_wx(p)
 
     @pl.when(early)
     def _():
-        for p in range(2, 4):
+        for p in range(4, 8):
             start_wa(p)
 
     low_t = from_t(low, lowx, low_sem)
@@ -263,7 +261,7 @@
 
     def lanes_in(j):
         first, size = chunks[j]
-        return pl.ds(n_x * first, padded(n_x * size))
+        return pl.ds(lane_at[j], padded(n_x * size))
 
     spans = {0: (0, 2 * rows), 1: (2 * rows, 2 * soon), 2: (0, 2 * (rows + soon))}
 
@@ -319,7 +317,7 @@
         first, size = chunks[j]
         wide = n_x * size
         top, tall = spans[kb]
-        lanes = pl.ds(n_x * first, wide)
+        lanes = pl.ds(lane_at[j], wide)
 
         @pl.when(uu == t)
         def _():
@@ -340,10 +338,12 @@
                             got_out[far * 2 + c, pl.ds(*half), lanes] = total.astype(BF16)
                         else:
                             scat[side * 2 + kc_, pl.ds(*half), lanes] = total.astype(BF16)
-                    if side or kc_:
+                    if side and deferred:
+                        deferred[0].append((uu, side, kc_, j))
+                    elif side or kc_:
                         scatter(side, kc_, j).start()
 
-    pending = []
+    pending, deferred = [], [[]]
 
     def go(kb, ku, j):
         new = run_unit(kb, ku, j)
@@ -366,7 +366,8 @@
             return carry
 
         lax.fori_loop(0, depth // kc, late_step, 0)
-        return jnp.transpose(late_sum[...])
+        flat = jnp.transpose(late_sum[...])
+        return [(lane_at[j], flat[:, n_x * at : n_x * (at + size)]) for j, (at, size) in enumerate(chunks)]
 
     def late_scatter(kc_):
         return send(
@@ -417,24 +418,20 @@
     back[...] = back_part
     for k in range(1, n_u):
         start(send(back, backx.at[k - 1], back_sem, (k - 1,), t_to[k]))
-    for n, step in enumerate(steps):
-        if n:
-            peer = moved(step)
-            start(send(ga.at[lax.div(place_of(peer), n_u)], gax.at[n], ga_sem, (n,), peer))
     back_b = from_t(back, backx, back_sem).astype(BF16)
     backs[c] = back_b
     for k in range(1, 4):
         peer = at(b=shift(b, k // 2, 2), core=shift(c, k % 2, 2))
         start(send(backs.at[c], backs.at[k // 2 * 2 + c], tok_sem, (k - 1,), peer))
 
-    for i in range(3, H_CHUNK):
+    for i in range(3, n_soon):
         start_h(i)
-    for p in range(4, n_pc):
+    for p in range(8, n_pc):
         start_wx(p)
 
     @pl.when(early)
     def _():
-        for p in range(4, n_pc):
+        for p in range(8, n_pc):
             start_wa(p)
 
     for i in range(2):
@@ -450,7 +447,7 @@
             send(got, got, wr_sem, (k - 1, m - 1, p), x_to[m]).start()
 
     for j in range(n_ch):
-        while passed[0] < H_CHUNK * (j + 1) // n_ch:
+        while passed[0] < n_soon * (j + 1) // n_ch:
             pass_h()
         for p in of_chunk(j):
             near(p)
@@ -472,13 +469,18 @@
                 pl.semaphore_wait(turn_sem, 1)
                 for p in range(n_pc):
                     start_wa(p)
-                for i in range(H_CHUNK, n_h):
+                for i in range(n_soon, n_h):
                     late_h(i).start()
 
         go(0, 0, j)
-    for i in range(H_CHUNK):
+    for i in range(n_soon):
         got = h_rows(1, 1 - c, i)
         send(got, got, hr_sem, (i,), core_peer).wait_recv()
+
+    for n, step in enumerate(steps):
+        if n:
+            peer = moved(step)
+            start(send(ga.at[lax.div(place_of(peer), n_u)], gax.at[n], ga_sem, (n,), peer))
 
     for k in range(1, 4):
         src = k // 2 * 2 + shift(c, k % 2, 2)
@@ -508,75 +510,13 @@
         return pl.ds(pl.multiple_of(lax.div(place_of(device) * share_b, size_b) * size_b, LANES), size_b)
 
     groups = [step for step in steps if step[1] == 0 and step[3] == 0]
-    def far_piece(k, p):
-        @pl.when(jnp.logical_not(early))
-        def _():
-            w_arrived(k, p)
-            if k == n_u - 1 and p == n_pc - 1:
-                turn(b_peer)
-
-    def far_ready(k, j):
-        for p in of_chunk(j):
-            for m in range(1, n_x):
-                got = w_rows(shift(u, n_u - k, n_u), shift(x, n_x - m, n_x), p)
-                send(got, got, wr_sem, (k - 1, m - 1, p), x_to[m]).wait_recv()
-
-    units = [(1, 0, j) for j in range(n_ch)]
-    for k in range(1, n_u):
-        for p in range(n_pc):
-            done = [j for j in range(n_ch) if max(of_chunk(j)) == p - 1]
-            if units and not (k == n_u - 1 and p == n_pc - 1):
-                go(*units.pop(0))
-            far_piece(k, p)
-            for j in done:
-                far_ready(k, j)
-                units.append((2, n_u - k, j))
-        if k == n_u - 1:
-            while units:
-                go(*units.pop(0))
-
-            @pl.when(early)
-            def _():
-                pl.semaphore_wait(turn_sem, 1)
-                for i in range(H_CHUNK, n_h):
-                    late_h(i).start()
-
-        far_ready(k, n_ch - 1)
-        units.append((2, n_u - k, n_ch - 1))
-    for unit in units:
-        go(*unit)
-    finish(*pending.pop())
-
-    for i in range(H_CHUNK, n_h):
-        pass_h()
-    for i in range(H_CHUNK, n_h):
-        got = h_rows(1, 1 - c, i)
-        send(got, got, hr_sem, (i,), core_peer).wait_recv()
-    for k in range(1, n_u):
-        if k > 1:
-            late_part(shift(t, k - 1, n_u)).wait_send()
-        late_out[:, 0 : n_x * cols] = late_unit(shift(t, k, n_u)).astype(BF16)
-        late_part(shift(t, k, n_u)).start()
-
-    def grad_late(i, carry):
-        at_k = pl.ds(pl.multiple_of(i * kc, LANES), kc)
-        gb[:, at_k] += grad_of(1, 1, at_k)
-        return carry
-
-    lax.fori_loop(0, depth // kc, grad_late, 0)
-    for n, step in enumerate(groups):
-        if n:
-            peer = moved(step)
-            start(send(gb.at[:, lanes_of(peer)], gbx.at[n], gb_sem, (n,), peer))
-    late_own[:, 0 : n_x * cols] = late_unit(t)
-
     def emit(bb, cc, j, half):
         first, size = chunks[j]
         span = pl.ds(*halves[half])
         for xx in range(n_x):
             i = block_of(bb, xx, cc)
             left = i * cols + first
-            lane = n_x * first + xx * size
+            lane = lane_at[j] + xx * size
             pre = got_out[bb * 2 + cc, span, lane : lane + size].astype(F32)
             low_half = low_b[halves[half][0] : sum(halves[half]), :]
             pre = pre + dot(low_half, pk_a[i, :, first : first + size], NN)
@@ -587,50 +527,124 @@
             else:
                 mg[i, 0:1, first : first + size] = part
 
-    def soon_outputs(bb):
-        for cc in range(2):
-            for j in range(n_ch):
-                kind = lax.rem(bb + far, 2) * 2 + lax.rem(cc + c, 2)
-
-                def scattered(span):
-                    got = got_out.at[bb * 2 + cc, span, lanes_in(j)]
-                    return send(got, got, sc_sem, (kind, j), core_peer)
-
-                @pl.when(jnp.logical_and(bb == far, cc != c))
-                def _():
-                    scattered(pl.ds(0, rows)).wait_recv()
-
-                @pl.when(bb != far)
-                def _():
-                    scattered(pl.ds(0, soon)).wait_recv()
-
-                emit(bb, cc, j, 0)
-
-                @pl.when(bb == far)
-                def _():
-                    emit(bb, cc, j, 1)
-
-    soon_outputs(0)
+    def scattered(bb, cc, j, span):
+        kind = lax.rem(bb + far, 2) * 2 + lax.rem(cc + c, 2)
+        got = got_out.at[bb * 2 + cc, span, lanes_in(j)]
+        return send(got, got, sc_sem, (kind, j), core_peer)
+
+    def near_outputs(which):
+        for bb in range(2):
+
+            @pl.when(bb == far)
+            def _():
+                for j in which:
+                    for cc in range(2):
+                        pl.when(cc != c)(scattered(bb, cc, j, pl.ds(0, rows)).wait_recv)
+                        for half in range(2):
+                            emit(bb, cc, j, half)
+
+    def far_outputs(which, half):
+        for bb in range(2):
+
+            @pl.when(bb != far)
+            def _():
+                for j in which:
+                    for cc in range(2):
+                        if half == 0:
+                            scattered(bb, cc, j, pl.ds(0, soon)).wait_recv()
+                        emit(bb, cc, j, half)
+
+    def far_piece(k, p):
+        @pl.when(jnp.logical_not(early))
+        def _():
+            w_arrived(k, p)
+            if k == n_u - 1 and p == n_pc - 1:
+                turn(b_peer)
+
+    def far_ready(k, j):
+        for p in of_chunk(j):
+            for m in range(1, n_x):
+                got = w_rows(shift(u, n_u - k, n_u), shift(x, n_x - m, n_x), p)
+                send(got, got, wr_sem, (k - 1, m - 1, p), x_to[m]).wait_recv()
+
+    units = [(1, 0, j) for j in range(n_ch)]
+    early_out = 2 if n_ch > 2 else 0
+
+    for k in range(1, n_u):
+        for p in range(n_pc):
+            if pending:
+                finish(*pending.pop())
+            elif units:
+                pending.append(run_unit(*units.pop(0)))
+            if k == n_u - 1 and n_ch > 2 and p == n_pc - 5:
+                near_outputs([0])
+            far_piece(k, p)
+            for j in range(n_ch - 1):
+                if max(of_chunk(j)) + 2 == p:
+                    far_ready(k, j)
+                    units += [(0, n_u - k, j), (1, n_u - k, j)]
+        if k == n_u - 1:
+
+            @pl.when(early)
+            def _():
+                pl.semaphore_wait(turn_sem, 1)
+                late_h(n_soon).start()
+
+        while units:
+            go(*units.pop(0))
+        if k == n_u - 1:
+            near_outputs(range(max(early_out - 1, 0), early_out))
+        for j in range(n_ch):
+            if max(of_chunk(j)) + 2 >= n_pc:
+                far_ready(k, j)
+                if k == n_u - 1 and deferred:
+                    for uu, side, kc_, i in deferred.pop():
+                        pl.when(uu == t)(scatter(side, kc_, i).start)
+                go(2, n_u - k, j)
+
+    for i in range(n_soon, n_h):
+        pass_h()
+    for i in range(n_soon, n_h):
+        got = h_rows(1, 1 - c, i)
+        send(got, got, hr_sem, (i,), core_peer).wait_recv()
+    for k in range(1, n_u):
+        if k > 1:
+            late_part(shift(t, k - 1, n_u)).wait_send()
+        for lane, part in late_unit(shift(t, k, n_u)):
+            late_out[:, lane : lane + part.shape[1]] = part.astype(BF16)
+        late_part(shift(t, k, n_u)).start()
+    finish(*pending.pop())
+
+    def grad_late(i, carry):
+        at_k = pl.ds(pl.multiple_of(i * kc, LANES), kc)
+        gb[:, at_k] += grad_of(1, 1, at_k)
+        return carry
+
+    lax.fori_loop(0, depth // kc, grad_late, 0)
+    for n, step in enumerate(groups):
+        if n:
+            peer = moved(step)
+            start(send(gb.at[:, lanes_of(peer)], gbx.at[n], gb_sem, (n,), peer))
+    for lane, part in late_unit(t):
+        late_own[:, lane : lane + part.shape[1]] = part
+
     for k in range(n_u - 1):
         remote(late_out, late_in.at[k], ls_sem.at[0], lr_sem.at[k], t_to[1]).wait_recv()
     for kc_ in range(2):
         at_c = pl.ds(pl.multiple_of(shift(c, kc_, 2) * late, 16), late)
-        total = late_own[at_c, 0 : n_x * cols]
-        for k in range(n_u - 1):
-            total = total + late_in[k, at_c, 0 : n_x * cols].astype(F32)
-        scat[2 + kc_, pl.ds(soon, late), 0 : n_x * cols] = total.astype(BF16)
+        for j, (_, size) in enumerate(chunks):
+            lanes = pl.ds(lane_at[j], n_x * size)
+            total = late_own[at_c, lanes]
+            for k in range(n_u - 1):
+                total = total + late_in[k, at_c, lanes].astype(F32)
+            scat[2 + kc_, pl.ds(soon, late), lanes] = total.astype(BF16)
         late_scatter(kc_).start()
-    soon_outputs(1)
+    near_outputs(range(early_out, n_ch))
+    far_outputs(range(n_ch), 0)
     for kc_ in range(2):
         got = got_out.at[(1 - far) * 2 + shift(c, kc_, 2), pl.ds(soon, late), :]
         send(got, got, lsc_sem, (kc_,), core_peer).wait_recv()
-    for bb in range(2):
-
-        @pl.when(bb != far)
-        def _():
-            for cc in range(2):
-                for j in range(n_ch):
-                    emit(bb, cc, j, 1)
+    far_outputs(range(n_ch), 1)
 
     for n, step in enumerate(steps):
         if n:
@@ -679,7 +693,7 @@
             got = w_rows(shift(u, n_u - k, n_u), x, p)
             for m in range(1, n_x):
                 send(got, got, wr_sem, (k - 1, m - 1, p), x_to[m]).wait_send()
-    for i in range(H_CHUNK, n_h):
+    for i in range(n_soon, n_h):
         late_h(i).wait_send()
     late_part(shift(t, n_u - 1, n_u)).wait_send()
     for kc_ in range(2):
@@ -710,11 +724,11 @@
     rank = factor_a.shape[0]
     n_blk = 4 * n_x
     n_dp = n_blk * n_u
-    n_ch, n_pc = len(chunks_of(cols, n_x)), len(pieces_of(cols, n_x))
+    n_ch, n_pc = len(chunks_of(cols, n_x)), len(cuts(cols, PIECE))
     wide = n_x * LANES
-    full = padded(n_x * cols)
+    full = sum(padded(n_x * size) for _, size in chunks_of(cols, n_x))
     late = rows // LATE_SHARE
-    n_h = H_CHUNK + LATE_CHUNK
+    n_h = len(cuts(rows - late, H_PIECE)) + 1
     size_b = granule(depth, n_dp)
     groups = n_u * n_x
     few = max(n_x - 1, 1)

time: 314 us -> 299 us (0.952)
  Pallas kernels: 305 us -> 289 us
    pallas_call x1, Pallas kernels: 305 us -> 289 us  [fused(): pl.pallas_call(functools.partial(kernel, n_u, n_x), out_shape=(jax.ShapeD...]
where the time goes in v4:
time: 299 us; the launch traced here: 295 us
  Pallas kernels  289 us (97%)
  local copies, waits for them, and re-layouts  5.7 us (2%)
    pallas_call x1, Pallas kernels, fused(): pl.pallas_call(functools.partial(kernel, n_u, n_x), out_shape=(jax.ShapeD...  289 us

profile of v4, /device:TPU:4, one launch (start us, length us, event | category | flops | bytes accessed | tf_op | source)
XLA Modules:
  0.0 294.9 jit_solution(8716276163019074720)
XLA Ops:
  0.6 1.3 broadcast_in_dim.3.mag
  1.9 288.5 %fused.1 = (bf16[320,2304]{1,0:T(8,128)(2,1)}, f32[1,144]{1,0:T(1,128)}, f32[16,144]{1,0:T(8,128)}, f32[16,576]{1,0:T(8,128)}) custom-call(bf16[320,9216]{1,0:T(8,128)(2,1)} %h.1, bf16[288,9216]{1,0:T(8,128)(2,1)} %bitcast.4, bf16[16,9216]{1,0:T(8,128)(2,1)} %bitcast.5, bf16[16,288]{1,0:T(8,128)(2,1)} %a.1, f32[1,2304]{1,0:T(1,128)} %broadcast_in_dim.3.mag, ...), custom_call_target="tpu_custom_call" | custom-call | tf_op jit(solution)/shard_map/fused/pallas_call | solution.py:738
  290.5 0.0 copy-start.2
  290.5 0.0 copy-start.1
  290.5 0.0 copy-start
  290.5 2.6 copy.14
  293.1 0.0 copy-done.2
  293.1 0.6 copy.15
  293.7 0.0 copy-done.1
  293.7 0.6 copy.16
  294.3 0.0 copy-done
  294.3 0.6 copy.17
Async XLA Ops:
  290.5 2.6 copy-start.2
  290.5 3.2 %copy-start.1 = (f32[16,144]{1,0:T(8,128)S(1)}, f32[16,144]{1,0:T(8,128)}, u32[]{:S(2)}) copy-start(f32[16,144]{1,0:T(8,128)} %get-tuple-element.18) | copy-start | bytes 27652
  290.5 3.8 %copy-start = (f32[16,576]{1,0:T(8,128)S(1)}, f32[16,576]{1,0:T(8,128)}, u32[]{:S(2)}) copy-start(f32[16,576]{1,0:T(8,128)} %get-tuple-element.11) | copy-start | bytes 110596

commit v5 on v4

--- a/solution.py
+++ b/solution.py
@@ -71,6 +71,7 @@
     late = rows // LATE_SHARE
     soon = rows - late
     kc = split_of(depth, 1152)
+    k_step = split_of(depth, 4608)
     h_cuts = cuts(soon, H_PIECE) + [(soon, late)]
     n_h = len(h_cuts)
     n_soon = n_h - 1
@@ -290,12 +291,12 @@
         own[place, 0:tall, 0:wide] = jnp.zeros((tall, wide), F32)
 
         def unit_step(i, carry):
-            at_k = pl.ds(pl.multiple_of(i * kc, LANES), kc)
+            at_k = pl.ds(pl.multiple_of(i * k_step, LANES), k_step)
             right = jnp.concatenate([ws[uu, xx, first : first + size, at_k] for xx in range(n_x)], axis=0)
             own[place, 0:tall, 0:wide] += dot(hs[top : top + tall, at_k], right, NT)
             return carry
 
-        lax.fori_loop(0, depth // kc, unit_step, 0)
+        lax.fori_loop(0, depth // k_step, unit_step, 0)
 
         @pl.when(jnp.logical_not(keep))
         def _():
@@ -358,14 +359,14 @@
         late_sum[...] = jnp.zeros(late_sum.shape, F32)
 
         def late_step(i, carry):
-            at_k = pl.ds(pl.multiple_of(i * kc, LANES), kc)
+            at_k = pl.ds(pl.multiple_of(i * k_step, LANES), k_step)
             right = jnp.concatenate(
                 [ws[uu, xx, first : first + size, at_k] for first, size in chunks for xx in range(n_x)], axis=0
             )
             late_sum[...] += dot(right, hs[2 * (rows + soon) : 4 * rows, at_k], NT)
             return carry
 
-        lax.fori_loop(0, depth // kc, late_step, 0)
+        lax.fori_loop(0, depth // k_step, late_step, 0)
         flat = jnp.transpose(late_sum[...])
         return [(lane_at[j], flat[:, n_x * at : n_x * (at + size)]) for j, (at, size) in enumerate(chunks)]
 
@@ -405,9 +406,11 @@
             else:
                 pl.when(u != t)(wait.wait_recv)
 
+    mag_row = jnp.concatenate([mag[i : i + 1, :] for i in range(mag.shape[0])], axis=1)
+
     def scale_of(i, first, size):
         norm = jnp.sqrt(pk_s[i, 0:1, first : first + size] + 1e-06)
-        return mag[:, i * cols + first : i * cols + first + size] / norm
+        return mag_row[:, i * cols + first : i * cols + first + size] / norm
 
     back_part = jnp.zeros((rank, rows), F32)
     for i in range(n_blk):
@@ -477,10 +480,6 @@
         got = h_rows(1, 1 - c, i)
         send(got, got, hr_sem, (i,), core_peer).wait_recv()
 
-    for n, step in enumerate(steps):
-        if n:
-            peer = moved(step)
-            start(send(ga.at[lax.div(place_of(peer), n_u)], gax.at[n], ga_sem, (n,), peer))
 
     for k in range(1, 4):
         src = k // 2 * 2 + shift(c, k % 2, 2)
@@ -639,6 +638,10 @@
                 total = total + late_in[k, at_c, lanes].astype(F32)
             scat[2 + kc_, pl.ds(soon, late), lanes] = total.astype(BF16)
         late_scatter(kc_).start()
+    for n, step in enumerate(steps):
+        if n:
+            peer = moved(step)
+            start(send(ga.at[lax.div(place_of(peer), n_u)], gax.at[n], ga_sem, (n,), peer))
     near_outputs(range(early_out, n_ch))
     far_outputs(range(n_ch), 0)
     for kc_ in range(2):
@@ -804,9 +807,13 @@
     )(hidden, weight_t, factor_bt, factor_a, magnitude, cotangent)
 
 
+def in_rows(values):
+    return values.reshape(-1, LANES) if values.shape[0] % LANES == 0 else values[None]
+
+
 def body(hidden, weight, factor_b, factor_a, magnitude, cotangent, *, n_u, n_x):
     mixed, mag, ga, gb = fused(
-        hidden, weight.T, factor_b.T, factor_a, magnitude[None], cotangent, n_u, n_x
+        hidden, weight.T, factor_b.T, factor_a, in_rows(magnitude), cotangent, n_u, n_x
     )
     return mixed, mag[0], ga, gb.T
 

time: 299 us -> 294 us (0.983)
  no operation moved by 1% of the time
where the time goes in v5:
time: 294 us; the launch traced here: 292 us
  Pallas kernels  287 us (98%)
  local copies, waits for them, and re-layouts  4.39 us (1%)
    pallas_call x1, Pallas kernels, fused(): pl.pallas_call(functools.partial(kernel, n_u, n_x), out_shape=(jax.ShapeD...  287 us

profile of v5, /device:TPU:4, one launch (start us, length us, event | category | flops | bytes accessed | tf_op | source)
XLA Modules:
  0.0 292.0 jit_solution(10229476236453761136)
XLA Ops:
  0.6 286.9 %fused.1 = (bf16[320,2304]{1,0:T(8,128)(2,1)}, f32[1,144]{1,0:T(1,128)}, f32[16,144]{1,0:T(8,128)}, f32[16,576]{1,0:T(8,128)}) custom-call(bf16[320,9216]{1,0:T(8,128)(2,1)} %h.1, bf16[288,9216]{1,0:T(8,128)(2,1)} %bitcast.5, bf16[16,9216]{1,0:T(8,128)(2,1)} %bitcast.6, bf16[16,288]{1,0:T(8,128)(2,1)} %a.1, f32[18,128]{1,0:T(8,128)} %bitcast.8, ...), custom_call_target="tpu_custom_call" | custom-call | tf_op jit(solution)/shard_map/fused/pallas_call | solution.py:741
  287.5 0.0 copy-start.2
  287.5 0.0 copy-start.1
  287.6 0.0 copy-start
  287.6 2.6 copy.14
  290.2 0.0 copy-done.2
  290.2 0.6 copy.15
  290.7 0.0 copy-done.1
  290.7 0.6 copy.16
  291.3 0.0 copy-done
  291.3 0.6 copy.17
Async XLA Ops:
  287.5 2.6 copy-start.2
  287.5 3.2 %copy-start.1 = (f32[16,144]{1,0:T(8,128)S(1)}, f32[16,144]{1,0:T(8,128)}, u32[]{:S(2)}) copy-start(f32[16,144]{1,0:T(8,128)} %get-tuple-element.18) | copy-start | bytes 27652
  287.6 3.8 %copy-start = (f32[16,576]{1,0:T(8,128)S(1)}, f32[16,576]{1,0:T(8,128)}, u32[]{:S(2)}) copy-start(f32[16,576]{1,0:T(8,128)} %get-tuple-element.11) | copy-start | bytes 110596
